TPU v7x, 32 devices: a 4x2x2 block of a 4x4x8 slice. The times are simulated.
32 devices in a mesh: batch: 4 (over y, z), group: 8 (over x, core).
Axes of the slice: x: 4, y: 2, z: 2, core: 2. Of those that a mesh axis runs over, the one named last changes fastest.
The devices are a block of a 4x4x8 slice.
Arguments:
- sort_keys: float32 [16384], P(('batch', 'group')), parts along dimension 0
- seg_ids: int32 [16384], P(('batch', 'group')), parts along dimension 0
- payload: bfloat16 [16384, 4096], P(('batch', 'group')), parts along dimension 0
Outputs:
- output: bfloat16 [16384, 4096], P(('batch', 'group')), parts along dimension 0
There are 4 independent parts. A program takes and returns all parts, laid end to end along the dimension named above; each array names one.
All inputs are finite; a program needn't handle non-finite values.
Results may differ from a plain program's by a relative error of at most 0.00654141.
Values are sent between devices in bfloat16 or wider.
A program may use at most 768 MiB of HBM per device.

v0:
```python
import jax
import jax.numpy as jnp
from jax import lax
from jax.sharding import PartitionSpec as P


def combine_runs(left_part, right_part):
    left_flag, left_rows = left_part
    right_flag, right_rows = right_part
    joined = jnp.where(right_flag[..., None], right_rows, left_rows + right_rows)
    return jnp.logical_or(left_flag, right_flag), joined


def solution(mesh):
    group_size = mesh.shape['group']

    def per_device(sort_keys, seg_ids, payload):
        rows_dev = sort_keys.shape[0]
        width = payload.shape[1]
        pair_rows = rows_dev // group_size
        capacity = 2 * pair_rows
        my_index = lax.axis_index('group')
        local_pos = jnp.arange(rows_dev, dtype=jnp.int32)
        sorted_keys, sorted_seg, local_order = lax.sort((sort_keys, seg_ids, local_pos), num_keys=1)
        samples = sorted_keys.reshape(group_size, pair_rows)[:, 0]
        all_samples = lax.all_gather(samples, 'group', tiled=True)
        ordered_samples = jnp.sort(all_samples)
        splitters = ordered_samples.reshape(group_size, group_size)[1:, group_size // 2]
        inner_starts = jnp.searchsorted(sorted_keys, splitters, side='left').astype(jnp.int32)
        bucket_start = jnp.concatenate([jnp.zeros((1,), jnp.int32), inner_starts])
        bucket_end = jnp.concatenate([inner_starts, jnp.full((1,), rows_dev, jnp.int32)])
        slot_ids = jnp.arange(capacity, dtype=jnp.int32)
        src_index = bucket_start[:, None] + slot_ids[None, :]
        in_bucket = src_index < bucket_end[:, None]
        src_clip = jnp.minimum(src_index, rows_dev - 1)
        send_keys = jnp.where(in_bucket, sorted_keys[src_clip], jnp.inf)
        send_seg = jnp.where(in_bucket, sorted_seg[src_clip], -1)
        send_rows = jnp.where(in_bucket[..., None], payload[local_order[src_clip]], 0)
        recv_keys = lax.all_to_all(send_keys, 'group', 0, 0, tiled=True)
        recv_seg = lax.all_to_all(send_seg, 'group', 0, 0, tiled=True)
        recv_rows = lax.all_to_all(send_rows, 'group', 0, 0, tiled=True)
        flat_count = group_size * capacity
        flat_pos = jnp.arange(flat_count, dtype=jnp.int32)
        merged_keys, merged_seg, merge_order = lax.sort(
            (recv_keys.reshape(flat_count), recv_seg.reshape(flat_count), flat_pos),
            num_keys=1, is_stable=True)
        merged_rows = recv_rows.reshape(flat_count, width)[merge_order].astype(jnp.float32)
        seg_change = merged_seg[1:] != merged_seg[:-1]
        run_start = jnp.concatenate([jnp.ones((1,), dtype=jnp.bool_), seg_change])
        _, local_scan = lax.associative_scan(combine_runs, (run_start, merged_rows))
        valid_count = jnp.sum(merged_keys < jnp.inf).astype(jnp.int32)
        break_pos = jnp.min(jnp.where(seg_change, flat_pos[1:], flat_count))
        inner_break = (break_pos < valid_count).astype(jnp.int32)
        last_slot = valid_count - 1
        summary_ids = jnp.stack([merged_seg[0], merged_seg[last_slot], inner_break])
        tail_sum = local_scan[last_slot]
        all_ids = lax.all_gather(summary_ids, 'group')
        all_tails = lax.all_gather(tail_sum, 'group')
        first_all = all_ids[:, 0]
        last_all = all_ids[:, 1]
        break_all = all_ids[:, 2]
        dev_ids = jnp.arange(group_size, dtype=jnp.int32)
        link_bad = jnp.concatenate(
            [jnp.ones((1,), jnp.int32), (last_all[:-1] != first_all[1:]).astype(jnp.int32)])
        bad_links = jnp.cumsum(link_bad)
        bad_inner = jnp.cumsum(break_all)
        prev_index = jnp.maximum(my_index - 1, 0)
        carry_mask = (dev_ids < my_index) & (bad_links[my_index] == bad_links) & (bad_inner[prev_index] == bad_inner)
        carry_in = jnp.dot(carry_mask.astype(jnp.float32), all_tails, preferred_element_type=jnp.float32)
        head_run = flat_pos < break_pos
        final_rows = (local_scan + jnp.where(head_run[:, None], carry_in[None, :], 0.0)).astype(jnp.bfloat16)
        _, undo_merge = lax.sort((merge_order, flat_pos), num_keys=1)
        reply = final_rows[undo_merge].reshape(group_size, capacity, width)
        returned = lax.all_to_all(reply, 'group', 0, 0, tiled=True)
        _, sorted_rank = lax.sort((local_order, local_pos), num_keys=1)
        bucket_of = jnp.searchsorted(inner_starts, sorted_rank, side='right').astype(jnp.int32)
        slot_of = bucket_of * capacity + sorted_rank - bucket_start[bucket_of]
        return returned.reshape(flat_count, width)[slot_of]

    row_spec = P(('batch', 'group'))
    mat_spec = P(('batch', 'group'), None)
    return jax.shard_map(per_device, mesh=mesh, in_specs=(row_spec, row_spec, mat_spec),
                         out_specs=mat_spec, check_vma=False)
```

profile of v0, /device:TPU:81, one launch (start us, length us, event | category | flops | bytes accessed | tf_op | source)
XLA Modules:
  0.0 890.0 jit_solution(13956417572414976923)
XLA Ops:
  0.0 4.1 sort.87
  6.6 13.8 %all-reduce.20 = f32[64]{0:T(128)S(1)} all-reduce(f32[64]{0:T(128)S(1)} %dynamic-update-slice), channel_id=2, replica_groups=mesh['batch'=4,'group'=8] {'group'}, use_global_device_ids=true, to_apply=%add.20 | all-reduce | flops 64 | bytes 512 | tf_op jit(solution)/shard_map/all_gather | solution.py:26
  22.8 7.4 while.48
  30.9 6.9 gather_fusion.3
  38.5 5.9 all-to-all-start.1
  44.4 6.9 gather_fusion.4
  52.0 6.9 gather_fusion.1
  58.9 17.8 %gather_fusion.2 = bf16[1024,4096]{1,0:T(8,128)(2,1)} fusion(bf16[512,4096]{1,0:T(8,128)(2,1)} %param.9, s32[1024]{0:T(1024)S(1)} %fusion.12), kind=kCustom, calls=%fused_computation.2 | custom fusion | bytes 16781312 | tf_op jit(solution)/shard_map/gather | solution.py:38
  76.7 4.9 all-to-all-start.2
  81.6 7.2 broadcast_select_fusion.2
  88.8 5.0 all-to-all-start
  110.2 79.0 %all-reduce.21 = s32[24]{0:T(128)S(1)} all-reduce(s32[24]{0:T(128)S(1)} %add_dynamic-update-slice_fusion), channel_id=3, replica_groups=mesh['batch'=4,'group'=8] {'group'}, use_global_device_ids=true, to_apply=%add.21 | all-reduce | flops 24 | bytes 192
  191.1 4.4 sort.90
  196.9 20.0 %gather_fusion.5 = bf16[1024,4096]{1,0:T(8,128)(2,1)} fusion(bf16[1024,4096]{1,0:T(8,128)(2,1)} %bitcast.5, s32[1024]{0:T(1024)S(1)} %fusion.13), kind=kCustom, calls=%fused_computation.5 | custom fusion | bytes 16781312 | tf_op jit(solution)/shard_map/gather | solution.py:47
  217.8 35.5 %slice.273 = f32[512,4096]{1,0:T(8,128)} slice(bf16[1024,4096]{1,0:T(8,128)(2,1)} %gather_fusion.5), slice={[0:1023:2], [0:4096:1]} | slice | bytes 16777216 | tf_op jit(solution)/shard_map/slice | solution.py:50
  253.2 35.5 %slice.272 = f32[512,4096]{1,0:T(8,128)} slice(bf16[1024,4096]{1,0:T(8,128)(2,1)} %gather_fusion.5), slice={[1:1024:2], [0:4096:1]} | slice | bytes 16777216 | tf_op jit(solution)/shard_map/slice | solution.py:50
  288.7 36.1 %slice.270 = f32[511,4096]{1,0:T(8,128)} slice(bf16[1024,4096]{1,0:T(8,128)(2,1)} %gather_fusion.5), slice={[2:1024:2], [0:4096:1]} | slice | bytes 16744448 | tf_op jit(solution)/shard_map/slice | solution.py:50
  324.7 11.7 %add_select_fusion.1 = f32[512,4096]{1,0:T(8,128)} fusion(f32[512,4096]{1,0:T(8,128)} %slice.272, f32[512,4096]{1,0:T(8,128)} %slice.273, pred[512]{0:T(512)(128)(4,1)S(1)} %slice.271), kind=kLoop, calls=%fused_computation.28 | loop fusion | flops 4194304 | bytes 25166336 | tf_op jit(solution)/shard_map/jit(_where)/select_n | solution.py:10
  336.5 18.5 %slice.280 = f32[256,4096]{1,0:T(8,128)} slice(f32[512,4096]{1,0:T(8,128)} %add_select_fusion.1), slice={[0:511:2], [0:4096:1]} | slice | bytes 8388608 | tf_op jit(solution)/shard_map/slice | solution.py:50
  355.0 18.5 %slice.279 = f32[256,4096]{1,0:T(8,128)} slice(f32[512,4096]{1,0:T(8,128)} %add_select_fusion.1), slice={[1:512:2], [0:4096:1]} | slice | bytes 8388608 | tf_op jit(solution)/shard_map/slice | solution.py:50
  373.5 18.9 %slice.277 = f32[255,4096]{1,0:T(8,128)} slice(f32[512,4096]{1,0:T(8,128)} %add_select_fusion.1), slice={[2:512:2], [0:4096:1]} | slice | bytes 8355840 | tf_op jit(solution)/shard_map/slice | solution.py:50
  392.4 4.3 add_select_fusion.3
  398.7 9.8 %slice.287 = f32[128,4096]{1,0:T(8,128)} slice(f32[256,4096]{1,0:T(8,128)} %copy-done.4), slice={[0:255:2], [0:4096:1]} | slice | bytes 4194304 | tf_op jit(solution)/shard_map/slice | solution.py:50
  408.5 9.8 %slice.286 = f32[128,4096]{1,0:T(8,128)} slice(f32[256,4096]{1,0:T(8,128)} %copy-done.4), slice={[1:256:2], [0:4096:1]} | slice | bytes 4194304 | tf_op jit(solution)/shard_map/slice | solution.py:50
  418.3 10.0 %slice.284 = f32[127,4096]{1,0:T(8,128)} slice(f32[256,4096]{1,0:T(8,128)} %copy-done.4), slice={[2:256:2], [0:4096:1]} | slice | bytes 4161536 | tf_op jit(solution)/shard_map/slice | solution.py:50
  454.8 4.2 pad.73
  459.0 4.9 pad.74
  469.5 16.6 %pad.75 = f32[256,4096]{1,0:T(8,128)} pad(f32[128,4096]{1,0:T(8,128)} %pad_maximum_fusion.2, f32[]{:T(128)} %constant.158.clone.1), padding=0_1_1x0_0_0 | pad | bytes 6291460 | tf_op jit(solution)/shard_map/pad | solution.py:50
  486.1 9.0 %pad.76 = f32[256,4096]{1,0:T(8,128)} pad(f32[128,4096]{1,0:T(8,128)S(1)} %copy-done.8, f32[]{:T(128)} %constant.158.clone.1), padding=1_0_1x0_0_0 | pad | bytes 6291460 | tf_op jit(solution)/shard_map/pad | solution.py:50
  495.1 6.4 add.291
  508.0 32.4 %pad.77 = f32[512,4096]{1,0:T(8,128)} pad(f32[256,4096]{1,0:T(8,128)} %pad_maximum_fusion.1, f32[]{:T(128)} %constant.158.clone.1), padding=0_1_1x0_0_0 | pad | bytes 12582916 | tf_op jit(solution)/shard_map/pad | solution.py:50
  540.4 32.5 %pad.78 = f32[512,4096]{1,0:T(8,128)} pad(f32[256,4096]{1,0:T(8,128)} %add.291, f32[]{:T(128)} %constant.158.clone.1), padding=1_0_1x0_0_0 | pad | bytes 12582916 | tf_op jit(solution)/shard_map/pad | solution.py:50
  572.8 11.1 %add.293 = f32[512,4096]{1,0:T(8,128)} add(f32[512,4096]{1,0:T(8,128)} %pad.77, f32[512,4096]{1,0:T(8,128)} %pad.78) | non-fusion elementwise | flops 2097152 | bytes 25165824 | tf_op jit(solution)/shard_map/add | solution.py:50
  583.9 9.7 %add_select_fusion = f32[511,4096]{1,0:T(8,128)S(1)} fusion(f32[511,4096]{1,0:T(8,128)} %slice.270, f32[512,4096]{1,0:T(8,128)} %pad.78, f32[512,4096]{1,0:T(8,128)} %pad.77, pred[511]{0:T(512)(128)(4,1)S(1)} %slice.269), kind=kLoop, calls=%fused_computation.27 | loop fusion | flops 6279168 | bytes 33489408 | tf_op jit(solution)/shard_map/jit(_where)/select_n | solution.py:10
  593.6 4.1 pad_maximum_fusion
  597.7 64.1 %pad.79 = f32[1024,4096]{1,0:T(8,128)} pad(f32[512,4096]{1,0:T(8,128)} %pad_maximum_fusion, f32[]{:T(128)} %constant.158.clone.1), padding=0_1_1x0_0_0 | pad | bytes 25165828 | tf_op jit(solution)/shard_map/pad | solution.py:50
  661.9 64.1 %pad.80 = f32[1024,4096]{1,0:T(8,128)} pad(f32[512,4096]{1,0:T(8,128)} %add.293, f32[]{:T(128)} %constant.158.clone.1), padding=1_0_1x0_0_0 | pad | bytes 25165828 | tf_op jit(solution)/shard_map/pad | solution.py:50
  727.0 14.9 %all-gather.2 = bf16[8,1,4096]{2,1,0:T(2,128)(2,1)S(1)} all-gather(bf16[1,1,4096]{2,1,0:T(2,128)(2,1)S(1)} %add_bitcast_fusion), channel_id=1, replica_groups=mesh['batch'=4,'group'=8] {'group'}, dimensions={0}, use_global_device_ids=true | all-gather | bytes 73728 | tf_op jit(solution)/shard_map/all_gather | solution.py:58
  742.7 15.2 %add_convert_fusion = bf16[1024,4096]{1,0:T(8,128)(2,1)} fusion(f32[1024,4096]{1,0:T(8,128)} %pad.79, f32[1024,4096]{1,0:T(8,128)} %pad.80, f32[4096]{0:T(1024)S(1)} %bitcast.73, pred[1024]{0:T(1024)(128)(4,1)S(1)} %iota_compare_fusion), kind=kLoop, calls=%fused_computation.26 | loop fusion | flops 16777216 | bytes 41960448 | tf_op jit(solution)/shard_map/convert_element_type | solution.py:71
  757.9 19.5 %gather_fusion.6 = bf16[1024,4096]{1,0:T(8,128)(2,1)} fusion(bf16[1024,4096]{1,0:T(8,128)(2,1)} %add_convert_fusion, s32[1024]{0:T(1024)S(1)} %fusion.14), kind=kCustom, calls=%fused_computation.6 | custom fusion | bytes 16781312 | tf_op jit(solution)/shard_map/gather | solution.py:73
  777.4 5.6 all-to-all-start.3
  787.5 15.1 %while.49 = (s32[]{:T(128)}, u32[512]{0:T(512)S(1)}, u32[512]{0:T(512)S(1)}, s32[7]{0:T(128)S(1)}, s32[512]{0:T(512)S(1)}, /*index=5*/s32[]{:T(128)}, s32[]{:T(128)}) while((s32[]{:T(128)}, u32[512]{0:T(512)S(1)}, u32[512]{0:T(512)S(1)}, s32[7]{0:T(128)S(1)}, s32[512]{0:T(512)S(1)}, /*index=5*/s32[]{:T(128)}, s32[]{:T(128)}) %tuple.86), condition=%wide.region_12.13_spmd.clone, body=%wide.region_11.12_spmd.clone.sunk | while | flops 12803 | bytes 19628 | solution.py:76
  788.2 4.3 select_select_fusion.4
  793.2 4.3 select_select_fusion.4
  798.2 4.3 select_select_fusion.4
  802.6 4.4 compare_select_fusion.11
  807.0 69.5 %all-to-all-done.3 = bf16[8,128,4096]{2,1,0:T(8,128)(2,1)} async-done(((bf16[8,128,4096]{2,1,0:T(8,128)(2,1)}), bf16[8,128,4096]{2,1,0:T(8,128)(2,1)}, u32[]{:S(2)}, u32[]{:S(2)}) %all-to-all-start.3) | async-done | bytes 8388640 | tf_op jit(solution)/shard_map/all_to_all | solution.py:74
  876.5 13.0 %gather_fusion.7 = bf16[512,4096]{1,0:T(8,128)(2,1)} fusion(bf16[1024,4096]{1,0:T(8,128)(2,1)} %bitcast.22, s32[1024]{0:T(1024)S(1)} %pad_clamp_fusion.1), kind=kCustom, calls=%fused_computation.7 | custom fusion | bytes 8390656 | tf_op jit(solution)/shard_map/gather | solution.py:78
  (259 shorter events, 78.9 us)
Async XLA Ops:
  4.1 47.8 %copy-start = (s32[512]{0:T(512)}, s32[512]{0:T(512)S(1)}, u32[]{:S(2)}) copy-start(s32[512]{0:T(512)S(1)} %get-tuple-element.154) | copy-start | bytes 6148
  30.2 0.6 copy-start.13
  38.5 38.2 %all-to-all-start.1 = ((f32[8,1,128]{2,1,0:T(1,128)}), f32[8,1,128]{2,1,0:T(1,128)S(1)}, u32[]{:S(2)}, u32[]{:S(2)}) async-start(f32[8,1,128]{2,1,0:T(1,128)} %compare_select_fusion.10), calls=%async_computation.1 | async-start | bytes 8192 | tf_op jit(solution)/shard_map/all_to_all | solution.py:39
  76.7 12.1 %all-to-all-start.2 = ((s32[8,1,128]{2,1,0:T(1,128)}), s32[8,1,128]{2,1,0:T(1,128)S(1)}, u32[]{:S(2)}, u32[]{:S(2)}) async-start(s32[8,1,128]{2,1,0:T(1,128)} %compare_select_fusion.9), calls=%async_computation.2 | async-start | bytes 8192 | tf_op jit(solution)/shard_map/all_to_all | solution.py:40
  88.8 108.1 %all-to-all-start = ((bf16[8,128,4096]{2,1,0:T(8,128)(2,1)}), bf16[8,128,4096]{2,1,0:T(8,128)(2,1)}, u32[]{:S(2)}, u32[]{:S(2)}) async-start(bf16[8,128,4096]{2,1,0:T(8,128)(2,1)} %broadcast_select_fusion.2), calls=%async_computation | async-start | bytes 16777216 | tf_op jit(solution)/shard_map/all_to_all | solution.py:41
  396.7 2.0 copy-start.4
  430.9 10.5 %copy-start.7 = (f32[128,4096]{1,0:T(8,128)}, f32[128,4096]{1,0:T(8,128)S(1)}, u32[]{:S(2)}) copy-start(f32[128,4096]{1,0:T(8,128)S(1)} %add_select_fusion.5) | copy-start | bytes 6291460
  441.4 4.4 copy-start.10
  448.5 1.4 slice-start.3
  449.9 3.5 copy-start.11
  450.2 3.6 slice-start.2
  453.7 5.3 copy-start.12
  463.9 3.3 copy-start.5
  463.9 3.3 copy-start.9
  467.2 0.7 slice-start.1
  469.5 16.6 %copy-start.8 = (f32[128,4096]{1,0:T(8,128)S(1)}, f32[128,4096]{1,0:T(8,128)}, u32[]{:S(2)}) copy-start(f32[128,4096]{1,0:T(8,128)} %add.289) | copy-start | bytes 6291460
  495.1 6.4 copy-start.2
  495.1 7.4 copy-start.3
  495.1 8.6 copy-start.6
  503.7 1.7 slice-start
  777.4 5.7 copy-start.1
  777.4 9.4 %copy-start.14 = (s32[7]{0:T(128)S(1)}, s32[7]{0:T(128)}, u32[]{:S(2)}) copy-start(s32[7]{0:T(128)} %copy-done.13) | copy-start | bytes 88
  777.4 99.1 %all-to-all-start.3 = ((bf16[8,128,4096]{2,1,0:T(8,128)(2,1)}), bf16[8,128,4096]{2,1,0:T(8,128)(2,1)}, u32[]{:S(2)}, u32[]{:S(2)}) async-start(bf16[8,128,4096]{2,1,0:T(8,128)(2,1)} %bitcast.71), calls=%async_computation.3 | async-start | bytes 16777216 | tf_op jit(solution)/shard_map/all_to_all | solution.py:74
where the time goes:
time: 907 us; the launch traced here: 890 us
  local copies, waits for them, and re-layouts  551 us (61%)
  other arithmetic  134 us (15%)
  blocking collectives  108 us (12%)
  waiting for transfers between devices  69.5 us (8%)
  starting transfers between devices  21.4 us (2%)
    pad x18, local copies, waits for them, and re-layouts, per_device(): _, local_scan = lax.associative_scan(combine_runs, (run_start, merged_rows))  230 us
    slice x66, local copies, waits for them, and re-layouts, per_device(): _, local_scan = lax.associative_scan(combine_runs, (run_start, merged_rows))  211 us
    unnamed x1, blocking collectives  79 us
    all_to_all x1, waiting for transfers between devices, per_device(): returned = lax.all_to_all(reply, 'group', 0, 0, tiled=True)  69.5 us
    select_n x17, other arithmetic, combine_runs(): jnp.where(right_flag[..., None], right_rows, left_rows + right_rows)  34.2 us
    add x9, other arithmetic, per_device(): _, local_scan = lax.associative_scan(combine_runs, (run_start, merged_rows))  22.9 us
    gather x1, local copies, waits for them, and re-layouts, per_device(): recv_rows.reshape(flat_count, width)[merge_order].astype(jnp.float32)  20 us
    gather x1, local copies, waits for them, and re-layouts, per_device(): reply = final_rows[undo_merge].reshape(group_size, capacity, width)  19.5 us
  transfers between devices with their start and end apart: 4, of which 1 were waited for; matrix products, arithmetic and copies ran while one was open for 9% of the time, Pallas kernels for 0%

commit v1 on v0

v1 whole, which is shorter than its diff:
```python
import functools

import jax
import jax.numpy as jnp
from jax import lax
from jax.experimental import pallas as pl
from jax.experimental.pallas import tpu as pltpu
from jax.sharding import PartitionSpec as P

MESH = pl.DeviceIdType.MESH
LANES = 128
CHUNKS = 2
ROW_TILE = 64
DOT_ROWS = 256


def exchange_kernel(n, keys_ref, segs_ref, pay_ref, out_ref, keys_all, segs_all, kcol, scol, mask, slab, res,
                    key_send, key_recv, seg_send, seg_recv, fwd_send, fwd_recv, ret_send, ret_recv):
    me = lax.axis_index('group')
    rows, width = pay_ref.shape
    block = width // n
    cw = block // CHUNKS
    halves = rows // DOT_ROWS
    lane_tiles = rows // LANES

    def peer(k):
        return lax.rem(me + k, n)

    order = [(k + n // 2) % n for k in range(n)]
    order = [k for k in order if k != 0]

    def key_copy(k):
        return pltpu.make_async_remote_copy(
            src_ref=keys_ref.at[0], dst_ref=keys_all.at[me], send_sem=key_send.at[k], recv_sem=key_recv.at[me],
            device_id={'group': peer(k)}, device_id_type=MESH)

    def seg_copy(k):
        return pltpu.make_async_remote_copy(
            src_ref=segs_ref.at[0], dst_ref=segs_all.at[me], send_sem=seg_send.at[k], recv_sem=seg_recv.at[me],
            device_id={'group': peer(k)}, device_id_type=MESH)

    def columns(dev, c):
        return pl.ds(pl.multiple_of(dev * block + c * cw, LANES), cw)

    def my_rows(dev):
        return pl.ds(pl.multiple_of(dev * rows, rows), rows)

    def fwd_copy(k, c):
        return pltpu.make_async_remote_copy(
            src_ref=pay_ref.at[:, columns(peer(k), c)], dst_ref=slab.at[c, my_rows(me), :],
            send_sem=fwd_send.at[k, c], recv_sem=fwd_recv.at[me, c],
            device_id={'group': peer(k)}, device_id_type=MESH)

    def ret_copy(dev, h, c):
        src_rows = pl.ds(pl.multiple_of(dev * rows + h * DOT_ROWS, DOT_ROWS), DOT_ROWS)
        dst_rows = pl.ds(pl.multiple_of(h * DOT_ROWS, DOT_ROWS), DOT_ROWS)
        return pltpu.make_async_remote_copy(
            src_ref=res.at[c, src_rows, :], dst_ref=out_ref.at[dst_rows, columns(me, c)],
            send_sem=ret_send.at[dev, c, h], recv_sem=ret_recv.at[me, c, h],
            device_id={'group': dev}, device_id_type=MESH)

    def ret_local(h, c):
        src_rows = pl.ds(pl.multiple_of(me * rows + h * DOT_ROWS, DOT_ROWS), DOT_ROWS)
        dst_rows = pl.ds(pl.multiple_of(h * DOT_ROWS, DOT_ROWS), DOT_ROWS)
        return pltpu.make_async_copy(res.at[c, src_rows, :], out_ref.at[dst_rows, columns(me, c)],
                                     ret_recv.at[me, c, h])

    own_copies = [pltpu.make_async_copy(keys_ref.at[0], keys_all.at[me], key_recv.at[me]),
                  pltpu.make_async_copy(segs_ref.at[0], segs_all.at[me], seg_recv.at[me])]
    own_copies += [pltpu.make_async_copy(pay_ref.at[:, columns(me, c)], slab.at[c, my_rows(me), :], fwd_recv.at[me, c])
                   for c in range(CHUNKS)]

    barrier = pltpu.get_barrier_semaphore()
    for k in range(1, n):
        pl.semaphore_signal(barrier, inc=1, device_id={'group': peer(k)}, device_id_type=MESH)
    for copy in own_copies:
        copy.start()
    pl.semaphore_wait(barrier, n - 1)

    for k in order:
        key_copy(k).start()
        seg_copy(k).start()
    for c in range(CHUNKS):
        for k in order:
            fwd_copy(k, c).start()

    own_copies[0].wait()
    own_copies[1].wait()
    for k in order:
        src = peer(k)
        pltpu.make_async_copy(keys_ref.at[0], keys_all.at[src], key_recv.at[src]).wait()
        pltpu.make_async_copy(segs_ref.at[0], segs_all.at[src], seg_recv.at[src]).wait()

    def spread(dev, carry):
        for j in range(lane_tiles):
            lanes = slice(j * LANES, (j + 1) * LANES)
            dst = pl.ds(pl.multiple_of(dev * rows + j * LANES, LANES), LANES)
            kcol[dst, :] = jnp.broadcast_to(keys_all[dev, :, lanes], (LANES, LANES)).T
            scol[dst, :] = jnp.broadcast_to(segs_all[dev, :, lanes], (LANES, LANES)).T
        return carry

    lax.fori_loop(0, n, spread, 0)

    def build(t, carry):
        here = pl.ds(pl.multiple_of(t * ROW_TILE, ROW_TILE), ROW_TILE)
        key_r, seg_r = kcol[here, :], scol[here, :]
        last = jnp.full((ROW_TILE, LANES), -jnp.inf, jnp.float32)
        for dev in range(n):
            for j in range(lane_tiles):
                lanes = slice(j * LANES, (j + 1) * LANES)
                key_s, seg_s = keys_all[dev, :, lanes], segs_all[dev, :, lanes]
                other = jnp.logical_and(key_s < key_r, seg_s != seg_r)
                last = jnp.maximum(last, jnp.where(other, key_s, -jnp.inf))
        last = jnp.broadcast_to(jnp.max(last, axis=1, keepdims=True), (ROW_TILE, LANES))
        for dev in range(n):
            for j in range(lane_tiles):
                lanes = slice(j * LANES, (j + 1) * LANES)
                key_s = keys_all[dev, :, lanes]
                inside = jnp.logical_and(key_s <= key_r, key_s > last)
                at = slice(dev * rows + j * LANES, dev * rows + (j + 1) * LANES)
                mask[here, at] = jnp.where(inside, 1.0, 0.0).astype(jnp.bfloat16)
        return carry

    lax.fori_loop(0, n * rows // ROW_TILE, build, 0)

    def send_back(step, c):
        dev = lax.rem(me + n // 2 + step // halves, n)
        h = lax.rem(step, halves)

        @pl.when(dev != me)
        def _():
            ret_copy(dev, h, c).start()

        @pl.when(dev == me)
        def _():
            ret_local(h, c).start()

    for c in range(CHUNKS):
        own_copies[2 + c].wait()
        for k in order:
            src = peer(k)
            pltpu.make_async_copy(pay_ref.at[:, columns(me, c)], slab.at[c, my_rows(src), :], fwd_recv.at[src, c]).wait()

        def dot_step(step, carry, c=c):
            dev = lax.rem(me + n // 2 + step // halves, n)
            at = pl.ds(pl.multiple_of(dev * rows + lax.rem(step, halves) * DOT_ROWS, DOT_ROWS), DOT_ROWS)
            total = jnp.dot(mask[at, :], slab[c], preferred_element_type=jnp.float32)
            res[c, at, :] = total.astype(jnp.bfloat16)

            @pl.when(step > 0)
            def _():
                send_back(step - 1, c)

            return carry

        lax.fori_loop(0, n * halves, dot_step, 0)
        send_back(n * halves - 1, c)

    for k in order:
        key_copy(k).wait_send()
        seg_copy(k).wait_send()
        for c in range(CHUNKS):
            fwd_copy(k, c).wait_send()
    for c in range(CHUNKS):
        for h in range(halves):
            for k in order:
                ret_copy(peer(k), h, c).wait_send()
            ret_local(h, c).wait()
            for k in order:
                src = peer(k)
                dst_rows = pl.ds(h * DOT_ROWS, DOT_ROWS)
                pltpu.make_async_copy(res.at[c, pl.ds(0, DOT_ROWS), :], out_ref.at[dst_rows, columns(src, c)],
                                      ret_recv.at[src, c, h]).wait()


def solution(mesh):
    n = mesh.shape['group']

    def per_device(sort_keys, seg_ids, payload):
        rows, width = payload.shape
        total = n * rows
        cw = width // n // CHUNKS
        halves = rows // DOT_ROWS
        dma = pltpu.SemaphoreType.DMA
        return pl.pallas_call(
            functools.partial(exchange_kernel, n),
            out_shape=jax.ShapeDtypeStruct((rows, width), jnp.bfloat16),
            in_specs=[pl.BlockSpec(memory_space=pl.ANY)] * 3,
            out_specs=pl.BlockSpec(memory_space=pl.ANY),
            scratch_shapes=[
                pltpu.VMEM((n, 1, rows), jnp.float32),
                pltpu.VMEM((n, 1, rows), jnp.int32),
                pltpu.VMEM((total, LANES), jnp.float32),
                pltpu.VMEM((total, LANES), jnp.int32),
                pltpu.VMEM((total, total), jnp.bfloat16),
                pltpu.VMEM((CHUNKS, total, cw), jnp.bfloat16),
                pltpu.VMEM((CHUNKS, total, cw), jnp.bfloat16),
                dma((n,)), dma((n,)), dma((n,)), dma((n,)),
                dma((n, CHUNKS)), dma((n, CHUNKS)),
                dma((n, CHUNKS, halves)), dma((n, CHUNKS, halves)),
            ],
            compiler_params=pltpu.CompilerParams(collective_id=0, has_side_effects=True,
                                                 vmem_limit_bytes=56 * 1024 * 1024),
            name='exchange_sums',
        )(sort_keys.reshape(1, 1, rows), seg_ids.reshape(1, 1, rows), payload)

    row_spec = P(('batch', 'group'))
    mat_spec = P(('batch', 'group'), None)
    return jax.shard_map(per_device, mesh=mesh, in_specs=(row_spec, row_spec, mat_spec),
                         out_specs=mat_spec, check_vma=False)
```

time: 907 us -> 102 us (0.11); the launches traced: 890 us -> 102 us
  local copies, waits for them, and re-layouts: 551 us -> 4.7 us
  other arithmetic: 134 us -> 0 us
  blocking collectives: 108 us -> 0 us
  Pallas kernels: 0 us -> 97.6 us
  waiting for transfers between devices: 69.5 us -> 0 us
  starting transfers between devices: 21.4 us -> 0 us
    pad x18 -> x0, local copies, waits for them, and re-layouts: 230 us -> none  [per_device(): _, local_scan = lax.associative_scan(combine_runs, (run_start, merged_rows))]
    slice x70 -> x0, local copies, waits for them, and re-layouts: 212 us -> none  [the longest x66 211 us: per_device(): _, local_scan = lax.associative_scan(combine_runs, (run_start, merged_rows))]
    gather x21 -> x0, local copies, waits for them, and re-layouts: 100 us -> none  [the longest x1 20 us: per_device(): recv_rows.reshape(flat_count, width)[merge_order].astype(jnp.float32)]
    pallas_call x0 -> x1, Pallas kernels: none -> 97.6 us  [per_device(): pl.pallas_call(functools.partial(exchange_kernel, n), out_shape=jax.Shape...]
    unnamed x1 -> x0, blocking collectives: 79 us -> none
    all_to_all x4 -> x0, waiting for transfers between devices: 69.5 us -> none  [the longest x1 69.5 us: per_device(): returned = lax.all_to_all(reply, 'group', 0, 0, tiled=True)]
    select_n x47 -> x0, other arithmetic: 60.4 us -> none  [the longest x17 34.2 us: combine_runs(): jnp.where(right_flag[..., None], right_rows, left_rows + right_rows)]
    all_gather x2 -> x0, blocking collectives: 28.7 us -> none  [the longest x1 14.9 us: per_device(): all_tails = lax.all_gather(tail_sum, 'group')]
  transfers between devices with their start and end apart: 4 -> 0, of which waited for: 1 -> 0; matrix products, arithmetic and copies ran while one was open for 9% -> 0% of each run, Pallas kernels for 0% -> 0%
where the time goes in v1:
time: 102 us
  Pallas kernels  97.6 us (96%)
  local copies, waits for them, and re-layouts  4.7 us (5%)
    pallas_call x1, Pallas kernels, per_device(): pl.pallas_call(functools.partial(exchange_kernel, n), out_shape=jax.Shape...  97.6 us
    unnamed x1, local copies, waits for them, and re-layouts  4.7 us

profile of v1, /device:TPU:81, one launch (start us, length us, event | category | flops | bytes accessed | tf_op | source)
XLA Modules:
  0.0 102.3 jit_solution(373904270994480198)
XLA Ops:
  0.0 97.6 %exchange_sums.1 = bf16[512,4096]{1,0:T(8,128)(2,1)} custom-call(f32[1,1,512]{2,1,0:T(1,128)} %bitcast.2, s32[1,1,512]{2,1,0:T(1,128)} %bitcast.3, bf16[512,4096]{1,0:T(8,128)(2,1)} %pay_ref.1), custom_call_target="tpu_custom_call" | custom-call | tf_op jit(solution)/shard_map/exchange_sums/pallas_call | solution.py:185
  97.6 4.7 %copy.5 = bf16[512,4096]{1,0:T(8,128)(2,1)} copy(bf16[512,4096]{1,0:T(8,128)(2,1)} %exchange_sums.1) | data formatting | bytes 8388608

commit v2 on v1

v2 whole, which is shorter than its diff:
```python
import functools

import jax
import jax.numpy as jnp
from jax import lax
from jax.experimental import pallas as pl
from jax.experimental.pallas import tpu as pltpu
from jax.sharding import PartitionSpec as P

MESH = pl.DeviceIdType.MESH
LANES = 128
CORES = 2
CHUNKS = 2
ROW_TILE = 64
DOT_ROWS = 256


def exchange_kernel(n, keys_ref, segs_ref, pay_ref, out_ref, keys_all, segs_all, kcol, scol, mask, pay, slab, res,
                    pay_sem, key_send, key_recv, seg_send, seg_recv, fwd_send, fwd_recv, ret_send, ret_recv):
    me = lax.axis_index('group')
    rows, width = pay_ref.shape
    block = width // n
    cw = block // CHUNKS
    halves = rows // DOT_ROWS
    lane_tiles = rows // LANES
    ring = n // CORES
    chip, core = lax.div(me, CORES), lax.rem(me, CORES)

    def peer(hop, flip):
        return lax.rem(chip + hop, ring) * CORES + lax.rem(core + flip, CORES)

    near = [(1, 0), (ring - 1, 0), (1, 1), (ring - 1, 1)]
    far = [(2, 0), (2, 1)]
    order = [peer(*p) for p in near + far + [(0, 1)]]

    def near_peer(i):
        return peer(1 + (ring - 2) * lax.rem(i, 2), lax.div(i, 2))

    def far_peer(i):
        return peer(2 + (ring - 2) * lax.div(i, 2), i + lax.div(i, 2))

    def key_copy(dst):
        return pltpu.make_async_remote_copy(
            src_ref=keys_ref.at[0], dst_ref=keys_all.at[me], send_sem=key_send.at[dst], recv_sem=key_recv.at[me],
            device_id={'group': dst}, device_id_type=MESH)

    def seg_copy(dst):
        return pltpu.make_async_remote_copy(
            src_ref=segs_ref.at[0], dst_ref=segs_all.at[me], send_sem=seg_send.at[dst], recv_sem=seg_recv.at[me],
            device_id={'group': dst}, device_id_type=MESH)

    def block_cols(dev):
        return pl.ds(pl.multiple_of(dev * block, LANES), block)

    def columns(dev, c):
        return pl.ds(pl.multiple_of(dev * block + c * cw, LANES), cw)

    def my_rows(dev):
        return pl.ds(pl.multiple_of(dev * rows, rows), rows)

    def pay_copy(dst):
        return pltpu.make_async_copy(pay_ref.at[:, block_cols(dst)], pay.at[:, block_cols(dst)], pay_sem.at[dst])

    def fwd_copy(dst, c):
        return pltpu.make_async_remote_copy(
            src_ref=pay.at[:, columns(dst, c)], dst_ref=slab.at[c, my_rows(me), :],
            send_sem=fwd_send.at[dst, c], recv_sem=fwd_recv.at[me, c],
            device_id={'group': dst}, device_id_type=MESH)

    def ret_copy(dev, h, c):
        src_rows = pl.ds(pl.multiple_of(dev * rows + h * DOT_ROWS, DOT_ROWS), DOT_ROWS)
        dst_rows = pl.ds(pl.multiple_of(h * DOT_ROWS, DOT_ROWS), DOT_ROWS)
        return pltpu.make_async_remote_copy(
            src_ref=res.at[c, src_rows, :], dst_ref=out_ref.at[dst_rows, columns(me, c)],
            send_sem=ret_send.at[dev, c, h], recv_sem=ret_recv.at[me, c, h],
            device_id={'group': dev}, device_id_type=MESH)

    own_copies = [pltpu.make_async_copy(keys_ref.at[0], keys_all.at[me], key_recv.at[me]),
                  pltpu.make_async_copy(segs_ref.at[0], segs_all.at[me], seg_recv.at[me])]
    own_copies += [pltpu.make_async_copy(pay_ref.at[:, columns(me, c)], slab.at[c, my_rows(me), :], fwd_recv.at[me, c])
                   for c in range(CHUNKS)]

    barrier = pltpu.get_barrier_semaphore()
    for dst in order:
        pl.semaphore_signal(barrier, inc=1, device_id={'group': dst}, device_id_type=MESH)
    for dst in order:
        pay_copy(dst).start()
    for copy in own_copies:
        copy.start()
    pl.semaphore_wait(barrier, n - 1)

    for dst in order:
        key_copy(dst).start()
        seg_copy(dst).start()
    for c in range(CHUNKS):
        for dst in order:
            if c == 0:
                pay_copy(dst).wait()
            fwd_copy(dst, c).start()

    own_copies[0].wait()
    own_copies[1].wait()
    for src in order:
        pltpu.make_async_copy(keys_ref.at[0], keys_all.at[src], key_recv.at[src]).wait()
        pltpu.make_async_copy(segs_ref.at[0], segs_all.at[src], seg_recv.at[src]).wait()

    def spread(dev, carry):
        for j in range(lane_tiles):
            lanes = slice(j * LANES, (j + 1) * LANES)
            dst = pl.ds(pl.multiple_of(dev * rows + j * LANES, LANES), LANES)
            kcol[dst, :] = jnp.broadcast_to(keys_all[dev, :, lanes], (LANES, LANES)).T
            scol[dst, :] = jnp.broadcast_to(segs_all[dev, :, lanes], (LANES, LANES)).T
        return carry

    lax.fori_loop(0, n, spread, 0)

    def build(t, carry):
        here = pl.ds(pl.multiple_of(t * ROW_TILE, ROW_TILE), ROW_TILE)
        key_r, seg_r = kcol[here, :], scol[here, :]
        last = jnp.full((ROW_TILE, LANES), -jnp.inf, jnp.float32)
        for dev in range(n):
            for j in range(lane_tiles):
                lanes = slice(j * LANES, (j + 1) * LANES)
                key_s, seg_s = keys_all[dev, :, lanes], segs_all[dev, :, lanes]
                other = jnp.logical_and(key_s < key_r, seg_s != seg_r)
                last = jnp.maximum(last, jnp.where(other, key_s, -jnp.inf))
        last = jnp.broadcast_to(jnp.max(last, axis=1, keepdims=True), (ROW_TILE, LANES))
        for dev in range(n):
            for j in range(lane_tiles):
                lanes = slice(j * LANES, (j + 1) * LANES)
                key_s = keys_all[dev, :, lanes]
                inside = jnp.logical_and(key_s <= key_r, key_s > last)
                at = slice(dev * rows + j * LANES, dev * rows + (j + 1) * LANES)
                mask[here, at] = jnp.where(inside, 1.0, 0.0).astype(jnp.bfloat16)
        return carry

    lax.fori_loop(0, n * rows // ROW_TILE, build, 0)

    def sums(dev, h, c):
        at = pl.ds(pl.multiple_of(dev * rows + h * DOT_ROWS, DOT_ROWS), DOT_ROWS)
        return jnp.dot(mask[at, :], slab[c], preferred_element_type=jnp.float32).astype(jnp.bfloat16)

    for c in range(CHUNKS):
        own_copies[2 + c].wait()
        for src in order:
            pltpu.make_async_copy(pay.at[:, columns(me, c)], slab.at[c, my_rows(src), :], fwd_recv.at[src, c]).wait()

        def dot_pass(pick, c=c):
            def dot_step(step, carry):
                dev, h = pick(lax.div(step, halves)), lax.rem(step, halves)
                at = pl.ds(pl.multiple_of(dev * rows + h * DOT_ROWS, DOT_ROWS), DOT_ROWS)
                res[c, at, :] = sums(dev, h, c)

                @pl.when(step > 0)
                def _():
                    ret_copy(pick(lax.div(step - 1, halves)), lax.rem(step - 1, halves), c).start()

                return carry
            return dot_step

        lax.fori_loop(0, 4 * halves, dot_pass(near_peer), 0)
        ret_copy(near_peer(3), halves - 1, c).start()
        lax.fori_loop(0, 3 * halves, dot_pass(far_peer), 0)
        ret_copy(far_peer(2), halves - 1, c).start()
        for h in range(halves):
            out_ref[pl.ds(h * DOT_ROWS, DOT_ROWS), columns(me, c)] = sums(me, h, c)

    for dst in order:
        key_copy(dst).wait_send()
        seg_copy(dst).wait_send()
        for c in range(CHUNKS):
            fwd_copy(dst, c).wait_send()
    for c in range(CHUNKS):
        for h in range(halves):
            for src in order:
                ret_copy(src, h, c).wait_send()
            for src in order:
                dst_rows = pl.ds(h * DOT_ROWS, DOT_ROWS)
                pltpu.make_async_copy(res.at[c, pl.ds(0, DOT_ROWS), :], out_ref.at[dst_rows, columns(src, c)],
                                      ret_recv.at[src, c, h]).wait()


def solution(mesh):
    n = mesh.shape['group']

    def per_device(sort_keys, seg_ids, payload):
        rows, width = payload.shape
        total = n * rows
        cw = width // n // CHUNKS
        halves = rows // DOT_ROWS
        dma = pltpu.SemaphoreType.DMA
        return pl.pallas_call(
            functools.partial(exchange_kernel, n),
            out_shape=pltpu.VMEM((rows, width), jnp.bfloat16),
            in_specs=[pl.BlockSpec(memory_space=pl.ANY)] * 3,
            out_specs=pl.BlockSpec(memory_space=pltpu.VMEM),
            scratch_shapes=[
                pltpu.VMEM((n, 1, rows), jnp.float32),
                pltpu.VMEM((n, 1, rows), jnp.int32),
                pltpu.VMEM((total, LANES), jnp.float32),
                pltpu.VMEM((total, LANES), jnp.int32),
                pltpu.VMEM((total, total), jnp.bfloat16),
                pltpu.VMEM((rows, width), jnp.bfloat16),
                pltpu.VMEM((CHUNKS, total, cw), jnp.bfloat16),
                pltpu.VMEM((CHUNKS, total, cw), jnp.bfloat16),
                dma((n,)), dma((n,)), dma((n,)), dma((n,)), dma((n,)),
                dma((n, CHUNKS)), dma((n, CHUNKS)),
                dma((n, CHUNKS, halves)), dma((n, CHUNKS, halves)),
            ],
            compiler_params=pltpu.CompilerParams(collective_id=0, has_side_effects=True,
                                                 vmem_limit_bytes=56 * 1024 * 1024),
            name='exchange_sums',
        )(sort_keys.reshape(1, 1, rows), seg_ids.reshape(1, 1, rows), payload)

    row_spec = P(('batch', 'group'))
    mat_spec = P(('batch', 'group'), None)
    return jax.shard_map(per_device, mesh=mesh, in_specs=(row_spec, row_spec, mat_spec),
                         out_specs=mat_spec, check_vma=False)
```

time: 102 us -> 100 us (0.980)
  local copies, waits for them, and re-layouts: 4.7 us -> 2.02 us
    unnamed x1, local copies, waits for them, and re-layouts: 4.7 us -> 2.02 us
where the time goes in v2:
time: 100 us
  Pallas kernels  98.1 us (98%)
  local copies, waits for them, and re-layouts  2.02 us (2%)
    pallas_call x1, Pallas kernels, per_device(): pl.pallas_call(functools.partial(exchange_kernel, n), out_shape=pltpu.VME...  98.1 us
    unnamed x1, local copies, waits for them, and re-layouts  2.02 us

profile of v2, /device:TPU:81, one launch (start us, length us, event | category | flops | bytes accessed | tf_op | source)
XLA Modules:
  0.0 100.2 jit_solution(14961766938487762267)
XLA Ops:
  0.0 98.1 %exchange_sums.1 = bf16[512,4096]{1,0:T(8,128)(2,1)S(1)} custom-call(f32[1,1,512]{2,1,0:T(1,128)} %bitcast.2, s32[1,1,512]{2,1,0:T(1,128)} %bitcast.3, bf16[512,4096]{1,0:T(8,128)(2,1)} %pay_ref.1), custom_call_target="tpu_custom_call" | custom-call | tf_op jit(solution)/shard_map/exchange_sums/pallas_call | solution.py:192
  98.1 2.0 %copy.5 = bf16[512,4096]{1,0:T(8,128)(2,1)} copy(bf16[512,4096]{1,0:T(8,128)(2,1)S(1)} %exchange_sums.1) | data formatting | bytes 8388608

commit v3 on v2

--- a/solution.py
+++ b/solution.py
@@ -16,7 +16,7 @@
 
 
 def exchange_kernel(n, keys_ref, segs_ref, pay_ref, out_ref, keys_all, segs_all, kcol, scol, mask, pay, slab, res,
-                    pay_sem, key_send, key_recv, seg_send, seg_recv, fwd_send, fwd_recv, ret_send, ret_recv):
+                    far_ok, pay_sem, key_send, key_recv, seg_send, seg_recv, fwd_send, fwd_recv, ret_send, ret_recv):
     me = lax.axis_index('group')
     rows, width = pay_ref.shape
     block = width // n
@@ -29,9 +29,9 @@
     def peer(hop, flip):
         return lax.rem(chip + hop, ring) * CORES + lax.rem(core + flip, CORES)
 
-    near = [(1, 0), (ring - 1, 0), (1, 1), (ring - 1, 1)]
-    far = [(2, 0), (2, 1)]
-    order = [peer(*p) for p in near + far + [(0, 1)]]
+    near = [peer(1, 0), peer(ring - 1, 0), peer(1, 1), peer(ring - 1, 1), peer(0, 1)]
+    far = [peer(2, 0), peer(2, 1)]
+    order = near + far
 
     def near_peer(i):
         return peer(1 + (ring - 2) * lax.rem(i, 2), lax.div(i, 2))
@@ -81,22 +81,37 @@
                    for c in range(CHUNKS)]
 
     barrier = pltpu.get_barrier_semaphore()
-    for dst in order:
+    for dst in near:
         pl.semaphore_signal(barrier, inc=1, device_id={'group': dst}, device_id_type=MESH)
     for dst in order:
         pay_copy(dst).start()
     for copy in own_copies:
         copy.start()
-    pl.semaphore_wait(barrier, n - 1)
-
-    for dst in order:
+    pl.semaphore_wait(barrier, len(near))
+    pl.semaphore_signal(far_ok, inc=1, device_id={'group': peer(ring - 1, 0)}, device_id_type=MESH)
+
+    for dst in near:
         key_copy(dst).start()
         seg_copy(dst).start()
+
+    def send_block(dst, c):
+        if c == 0:
+            pay_copy(dst).wait()
+        fwd_copy(dst, c).start()
+
+    for dst in near[:2]:
+        send_block(dst, 0)
+    pl.semaphore_wait(far_ok, 1)
+    for dst in far:
+        key_copy(dst).start()
+        seg_copy(dst).start()
+    for dst in near[2:]:
+        send_block(dst, 0)
+    for dst in near:
+        send_block(dst, 1)
     for c in range(CHUNKS):
-        for dst in order:
-            if c == 0:
-                pay_copy(dst).wait()
-            fwd_copy(dst, c).start()
+        for dst in far:
+            send_block(dst, c)
 
     own_copies[0].wait()
     own_copies[1].wait()
@@ -145,23 +160,31 @@
         for src in order:
             pltpu.make_async_copy(pay.at[:, columns(me, c)], slab.at[c, my_rows(src), :], fwd_recv.at[src, c]).wait()
 
-        def dot_pass(pick, c=c):
+        def dot_pass(pick, send, c=c):
             def dot_step(step, carry):
                 dev, h = pick(lax.div(step, halves)), lax.rem(step, halves)
                 at = pl.ds(pl.multiple_of(dev * rows + h * DOT_ROWS, DOT_ROWS), DOT_ROWS)
                 res[c, at, :] = sums(dev, h, c)
 
-                @pl.when(step > 0)
-                def _():
-                    ret_copy(pick(lax.div(step - 1, halves)), lax.rem(step - 1, halves), c).start()
+                if send:
+                    @pl.when(step > 0)
+                    def _():
+                        ret_copy(pick(lax.div(step - 1, halves)), lax.rem(step - 1, halves), c).start()
 
                 return carry
             return dot_step
 
-        lax.fori_loop(0, 4 * halves, dot_pass(near_peer), 0)
+        last_chunk = c == CHUNKS - 1
+        lax.fori_loop(0, 4 * halves, dot_pass(near_peer, True), 0)
         ret_copy(near_peer(3), halves - 1, c).start()
-        lax.fori_loop(0, 3 * halves, dot_pass(far_peer), 0)
-        ret_copy(far_peer(2), halves - 1, c).start()
+        if last_chunk:
+            for early in range(c):
+                for i in range(3):
+                    for h in range(halves):
+                        ret_copy(far_peer(i), h, early).start()
+        lax.fori_loop(0, 3 * halves, dot_pass(far_peer, last_chunk), 0)
+        if last_chunk:
+            ret_copy(far_peer(2), halves - 1, c).start()
         for h in range(halves):
             out_ref[pl.ds(h * DOT_ROWS, DOT_ROWS), columns(me, c)] = sums(me, h, c)
 
@@ -203,7 +226,7 @@
                 pltpu.VMEM((rows, width), jnp.bfloat16),
                 pltpu.VMEM((CHUNKS, total, cw), jnp.bfloat16),
                 pltpu.VMEM((CHUNKS, total, cw), jnp.bfloat16),
-                dma((n,)), dma((n,)), dma((n,)), dma((n,)), dma((n,)),
+                pltpu.SemaphoreType.REGULAR, dma((n,)), dma((n,)), dma((n,)), dma((n,)), dma((n,)),
                 dma((n, CHUNKS)), dma((n, CHUNKS)),
                 dma((n, CHUNKS, halves)), dma((n, CHUNKS, halves)),
             ],

time: 100 us -> 100 us (level)
  no operation moved by 1% of the time
where the time goes in v3:
time: 100 us
  Pallas kernels  98 us (98%)
  local copies, waits for them, and re-layouts  2.02 us (2%)
    pallas_call x1, Pallas kernels, per_device(): pl.pallas_call(functools.partial(exchange_kernel, n), out_shape=pltpu.VME...  98 us
    unnamed x1, local copies, waits for them, and re-layouts  2.02 us

profile of v3, /device:TPU:81, one launch (start us, length us, event | category | flops | bytes accessed | tf_op | source)
XLA Modules:
  0.0 100.1 jit_solution(8590810101895954581)
XLA Ops:
  0.0 98.0 %exchange_sums.1 = bf16[512,4096]{1,0:T(8,128)(2,1)S(1)} custom-call(f32[1,1,512]{2,1,0:T(1,128)} %bitcast.2, s32[1,1,512]{2,1,0:T(1,128)} %bitcast.3, bf16[512,4096]{1,0:T(8,128)(2,1)} %pay_ref.1), custom_call_target="tpu_custom_call" | custom-call | tf_op jit(solution)/shard_map/exchange_sums/pallas_call | solution.py:215
  98.1 2.0 %copy.5 = bf16[512,4096]{1,0:T(8,128)(2,1)} copy(bf16[512,4096]{1,0:T(8,128)(2,1)S(1)} %exchange_sums.1) | data formatting | bytes 8388608

commit v4 on v2

v4 whole, which is shorter than its diff:
```python
import functools

import jax
import jax.numpy as jnp
from jax import lax
from jax.experimental import pallas as pl
from jax.experimental.pallas import tpu as pltpu
from jax.sharding import PartitionSpec as P

MESH = pl.DeviceIdType.MESH
LANES = 128
CORES = 2
WAYS = 2
CHUNKS = 2
ROW_TILE = 64
EARLY_STEPS = 16


def exchange_kernel(n, keys_ref, segs_ref, pay_ref, out_ref, keys_all, segs_all, kcol, scol, mask, pay, slab, res,
                    relay, relay_back, far_ok, pay_sem, key_send, key_recv, seg_send, seg_recv, fwd_send, fwd_recv,
                    hop_send, hop_recv, on_send, far_recv, ret_send, ret_recv, back_send, back_recv, back_on_send):
    me = lax.axis_index('group')
    rows, width = pay_ref.shape
    block = width // n
    cw = block // CHUNKS
    half = rows // WAYS
    lane_tiles = rows // LANES
    ring = n // CORES
    chip, core = lax.div(me, CORES), lax.rem(me, CORES)

    def peer(hop, flip):
        return lax.rem(chip + hop, ring) * CORES + lax.rem(core + flip, CORES)

    def way(i):
        return 1 + (ring - 2) * i

    near = [peer(way(i), flip) for flip in range(CORES) for i in range(WAYS)] + [peer(0, 1)]
    far = [peer(2, flip) for flip in range(CORES)]
    both = [(i, flip) for flip in range(CORES) for i in range(WAYS)]

    def remote(src, dst, send_sem, recv_sem, dev):
        return pltpu.make_async_remote_copy(src_ref=src, dst_ref=dst, send_sem=send_sem, recv_sem=recv_sem,
                                            device_id={'group': dev}, device_id_type=MESH)

    def columns(dev, c):
        return pl.ds(pl.multiple_of(dev * block + c * cw, LANES), cw)

    def dev_rows(dev):
        return pl.ds(pl.multiple_of(dev * rows, rows), rows)

    def half_rows(dev, i):
        return pl.ds(pl.multiple_of(dev * rows + i * half, half), half)

    def key_copy(dst):
        return remote(keys_ref.at[0], keys_all.at[me], key_send.at[dst], key_recv.at[me], dst)

    def seg_copy(dst):
        return remote(segs_ref.at[0], segs_all.at[me], seg_send.at[dst], seg_recv.at[me], dst)

    def pay_copy(dst):
        cols = pl.ds(pl.multiple_of(dst * block, LANES), block)
        return pltpu.make_async_copy(pay_ref.at[:, cols], pay.at[:, cols], pay_sem.at[dst])

    def fwd_copy(dst, c):
        return remote(pay.at[:, columns(dst, c)], slab.at[c, dev_rows(me), :], fwd_send.at[dst, c], fwd_recv.at[me, c], dst)

    def hop_out(i, flip, c):
        return remote(pay.at[half_rows(0, i), columns(peer(2, flip), c)], relay.at[i, c, flip],
                      hop_send.at[i, c, flip], hop_recv.at[i, c, flip], peer(way(i), 0))

    def hop_on(i, flip, c):
        origin = peer(way(1 - i), 0)
        return remote(relay.at[i, c, flip], slab.at[c, half_rows(origin, i), :],
                      on_send.at[i, c, flip], far_recv.at[origin, c, i], peer(way(i), flip))

    def ret_copy(dst, i, c):
        return remote(res.at[c, half_rows(dst, i), :], out_ref.at[half_rows(0, i), columns(me, c)],
                      ret_send.at[dst, c, i], ret_recv.at[me, c, i], dst)

    def back_out(i, flip, c):
        return remote(res.at[c, half_rows(peer(2, flip), i), :], relay_back.at[i, c, flip],
                      back_send.at[i, c, flip], back_recv.at[i, c, flip], peer(way(i), 0))

    def back_on(i, flip, c):
        origin = peer(way(1 - i), 0)
        return remote(relay_back.at[i, c, flip], out_ref.at[half_rows(0, i), columns(origin, c)],
                      back_on_send.at[i, c, flip], ret_recv.at[origin, c, i], peer(way(i), flip))

    def arrived(dst, sem):
        pltpu.make_async_copy(dst, dst, sem).wait()

    own_copies = [pltpu.make_async_copy(keys_ref.at[0], keys_all.at[me], key_recv.at[me]),
                  pltpu.make_async_copy(segs_ref.at[0], segs_all.at[me], seg_recv.at[me])]
    own_copies += [pltpu.make_async_copy(pay_ref.at[:, columns(me, c)], slab.at[c, dev_rows(me), :], fwd_recv.at[me, c])
                   for c in range(CHUNKS)]

    barrier = pltpu.get_barrier_semaphore()
    for dst in near:
        pl.semaphore_signal(barrier, inc=1, device_id={'group': dst}, device_id_type=MESH)
    for dst in far + near:
        pay_copy(dst).start()
    for copy in own_copies:
        copy.start()
    pl.semaphore_wait(barrier, len(near))
    pl.semaphore_signal(far_ok, inc=1, device_id={'group': peer(way(1), 0)}, device_id_type=MESH)

    for dst in near:
        key_copy(dst).start()
        seg_copy(dst).start()
    for dst in far:
        pay_copy(dst).wait()
    for i, flip in both:
        hop_out(i, flip, 0).start()
    pl.semaphore_wait(far_ok, 1)
    for dst in far:
        key_copy(dst).start()
        seg_copy(dst).start()
    for dst in near:
        pay_copy(dst).wait()
        fwd_copy(dst, 0).start()

    own_copies[0].wait()
    own_copies[1].wait()
    for src in far + near:
        arrived(keys_all.at[src], key_recv.at[src])
        arrived(segs_all.at[src], seg_recv.at[src])

    def spread(dev, carry):
        for j in range(lane_tiles):
            lanes = slice(j * LANES, (j + 1) * LANES)
            dst = pl.ds(pl.multiple_of(dev * rows + j * LANES, LANES), LANES)
            kcol[dst, :] = jnp.broadcast_to(keys_all[dev, :, lanes], (LANES, LANES)).T
            scol[dst, :] = jnp.broadcast_to(segs_all[dev, :, lanes], (LANES, LANES)).T
        return carry

    lax.fori_loop(0, n, spread, 0)

    def build(t, carry):
        here = pl.ds(pl.multiple_of(t * ROW_TILE, ROW_TILE), ROW_TILE)
        key_r, seg_r = kcol[here, :], scol[here, :]
        last = jnp.full((ROW_TILE, LANES), -jnp.inf, jnp.float32)
        for dev in range(n):
            for j in range(lane_tiles):
                lanes = slice(j * LANES, (j + 1) * LANES)
                key_s, seg_s = keys_all[dev, :, lanes], segs_all[dev, :, lanes]
                other = jnp.logical_and(key_s < key_r, seg_s != seg_r)
                last = jnp.maximum(last, jnp.where(other, key_s, -jnp.inf))
        last = jnp.broadcast_to(jnp.max(last, axis=1, keepdims=True), (ROW_TILE, LANES))
        for dev in range(n):
            for j in range(lane_tiles):
                lanes = slice(j * LANES, (j + 1) * LANES)
                key_s = keys_all[dev, :, lanes]
                inside = jnp.logical_and(key_s <= key_r, key_s > last)
                at = slice(dev * rows + j * LANES, dev * rows + (j + 1) * LANES)
                mask[here, at] = jnp.where(inside, 1.0, 0.0).astype(jnp.bfloat16)
        return carry

    steps = n * rows // ROW_TILE
    for c in range(CHUNKS):
        lax.fori_loop(EARLY_STEPS * c, EARLY_STEPS * (c + 1) if c < CHUNKS - 1 else steps, build, 0)
        for i, flip in both:
            arrived(relay.at[i, c, flip], hop_recv.at[i, c, flip])
            hop_on(i, flip, c).start()
        if c + 1 < CHUNKS:
            for i, flip in both:
                hop_out(i, flip, c + 1).start()
            for dst in near:
                fwd_copy(dst, c + 1).start()

    def sums(dev, i, c):
        return jnp.dot(mask[half_rows(dev, i), :], slab[c], preferred_element_type=jnp.float32).astype(jnp.bfloat16)

    def near_pick(k):
        return peer(way(lax.rem(k, WAYS)), lax.div(k, WAYS))

    for c in range(CHUNKS):
        own_copies[2 + c].wait()
        for src in near:
            arrived(slab.at[c, dev_rows(src), :], fwd_recv.at[src, c])
        for src in far:
            for i in range(WAYS):
                arrived(slab.at[c, half_rows(src, i), :], far_recv.at[src, c, i])

        def far_step(step, carry, c=c):
            i, flip = lax.rem(step, WAYS), lax.div(step, WAYS)
            dev = peer(2, flip)
            res[c, half_rows(dev, i), :] = sums(dev, i, c)

            @pl.when(step > 0)
            def _():
                back_out(lax.rem(step - 1, WAYS), lax.div(step - 1, WAYS), c).start()

            return carry

        def near_step(step, carry, c=c):
            i, k = lax.rem(step, WAYS), lax.div(step, WAYS)
            dev = near_pick(k)
            res[c, half_rows(dev, i), :] = sums(dev, i, c)

            @pl.when(step == 0)
            def _():
                back_out(WAYS - 1, CORES - 1, c).start()

            @pl.when(step > 0)
            def _():
                ret_copy(near_pick(lax.div(step - 1, WAYS)), lax.rem(step - 1, WAYS), c).start()

            return carry

        def chip_step(i, carry, c=c):
            dev = peer(0, 1)
            res[c, half_rows(dev, i), :] = sums(dev, i, c)

            @pl.when(i == 0)
            def _():
                ret_copy(near[-2], WAYS - 1, c).start()

            @pl.when(i > 0)
            def _():
                ret_copy(dev, i - 1, c).start()

            return carry

        def own_step(i, carry, c=c):
            out_ref[half_rows(0, i), columns(me, c)] = sums(me, i, c)

            @pl.when(i == 0)
            def _():
                ret_copy(peer(0, 1), WAYS - 1, c).start()

            return carry

        lax.fori_loop(0, CORES * WAYS, far_step, 0)
        lax.fori_loop(0, CORES * WAYS * WAYS, near_step, 0)
        lax.fori_loop(0, WAYS, chip_step, 0)
        lax.fori_loop(0, WAYS, own_step, 0)

    for c in range(CHUNKS):
        for i, flip in both:
            arrived(relay_back.at[i, c, flip], back_recv.at[i, c, flip])
            back_on(i, flip, c).start()

    for dst in far + near:
        key_copy(dst).wait_send()
        seg_copy(dst).wait_send()
    for c in range(CHUNKS):
        for dst in near:
            fwd_copy(dst, c).wait_send()
            for i in range(WAYS):
                ret_copy(dst, i, c).wait_send()
        for i, flip in both:
            hop_out(i, flip, c).wait_send()
            hop_on(i, flip, c).wait_send()
            back_out(i, flip, c).wait_send()
        for src in near + far:
            for i in range(WAYS):
                arrived(out_ref.at[half_rows(0, i), columns(src, c)], ret_recv.at[src, c, i])
    for c in range(CHUNKS):
        for i, flip in both:
            back_on(i, flip, c).wait_send()


def solution(mesh):
    n = mesh.shape['group']

    def per_device(sort_keys, seg_ids, payload):
        rows, width = payload.shape
        total = n * rows
        cw = width // n // CHUNKS
        dma = pltpu.SemaphoreType.DMA
        hops = (WAYS, CHUNKS, CORES)
        return pl.pallas_call(
            functools.partial(exchange_kernel, n),
            out_shape=pltpu.VMEM((rows, width), jnp.bfloat16),
            in_specs=[pl.BlockSpec(memory_space=pl.ANY)] * 3,
            out_specs=pl.BlockSpec(memory_space=pltpu.VMEM),
            scratch_shapes=[
                pltpu.VMEM((n, 1, rows), jnp.float32),
                pltpu.VMEM((n, 1, rows), jnp.int32),
                pltpu.VMEM((total, LANES), jnp.float32),
                pltpu.VMEM((total, LANES), jnp.int32),
                pltpu.VMEM((total, total), jnp.bfloat16),
                pltpu.VMEM((rows, width), jnp.bfloat16),
                pltpu.VMEM((CHUNKS, total, cw), jnp.bfloat16),
                pltpu.VMEM((CHUNKS, total, cw), jnp.bfloat16),
                pltpu.VMEM((*hops, rows // WAYS, cw), jnp.bfloat16),
                pltpu.VMEM((*hops, rows // WAYS, cw), jnp.bfloat16),
                pltpu.SemaphoreType.REGULAR, dma((n,)), dma((n,)), dma((n,)), dma((n,)), dma((n,)),
                dma((n, CHUNKS)), dma((n, CHUNKS)),
                dma(hops), dma(hops), dma(hops), dma((n, CHUNKS, WAYS)),
                dma((n, CHUNKS, WAYS)), dma((n, CHUNKS, WAYS)), dma(hops), dma(hops), dma(hops),
            ],
            compiler_params=pltpu.CompilerParams(collective_id=0, has_side_effects=True,
                                                 vmem_limit_bytes=56 * 1024 * 1024),
            name='exchange_sums',
        )(sort_keys.reshape(1, 1, rows), seg_ids.reshape(1, 1, rows), payload)

    row_spec = P(('batch', 'group'))
    mat_spec = P(('batch', 'group'), None)
    return jax.shard_map(per_device, mesh=mesh, in_specs=(row_spec, row_spec, mat_spec),
                         out_specs=mat_spec, check_vma=False)
```

time: 100 us -> 100 us (level)
  no operation moved by 1% of the time
where the time goes in v4:
time: 100 us
  Pallas kernels  98 us (98%)
  local copies, waits for them, and re-layouts  2.02 us (2%)
    pallas_call x1, Pallas kernels, per_device(): pl.pallas_call(functools.partial(exchange_kernel, n), out_shape=pltpu.VME...  98 us
    unnamed x1, local copies, waits for them, and re-layouts  2.02 us

profile of v4, /device:TPU:81, one launch (start us, length us, event | category | flops | bytes accessed | tf_op | source)
XLA Modules:
  0.0 100.0 jit_solution(1160370040509028974)
XLA Ops:
  0.0 98.0 %exchange_sums.1 = bf16[512,4096]{1,0:T(8,128)(2,1)S(1)} custom-call(f32[1,1,512]{2,1,0:T(1,128)} %bitcast.2, s32[1,1,512]{2,1,0:T(1,128)} %bitcast.3, bf16[512,4096]{1,0:T(8,128)(2,1)} %pay_ref.1), custom_call_target="tpu_custom_call" | custom-call | tf_op jit(solution)/shard_map/exchange_sums/pallas_call | solution.py:272
  98.0 2.0 %copy.5 = bf16[512,4096]{1,0:T(8,128)(2,1)} copy(bf16[512,4096]{1,0:T(8,128)(2,1)S(1)} %exchange_sums.1) | data formatting | bytes 8388608

commit v5 on v4

--- a/solution.py
+++ b/solution.py
@@ -52,14 +52,13 @@
         return pl.ds(pl.multiple_of(dev * rows + i * half, half), half)
 
     def key_copy(dst):
-        return remote(keys_ref.at[0], keys_all.at[me], key_send.at[dst], key_recv.at[me], dst)
+        return remote(keys_all.at[me], keys_all.at[me], key_send.at[dst], key_recv.at[me], dst)
 
     def seg_copy(dst):
-        return remote(segs_ref.at[0], segs_all.at[me], seg_send.at[dst], seg_recv.at[me], dst)
-
-    def pay_copy(dst):
-        cols = pl.ds(pl.multiple_of(dst * block, LANES), block)
-        return pltpu.make_async_copy(pay_ref.at[:, cols], pay.at[:, cols], pay_sem.at[dst])
+        return remote(segs_all.at[me], segs_all.at[me], seg_send.at[dst], seg_recv.at[me], dst)
+
+    def pay_copy(dst, c):
+        return pltpu.make_async_copy(pay_ref.at[:, columns(dst, c)], pay.at[:, columns(dst, c)], pay_sem.at[dst, c])
 
     def fwd_copy(dst, c):
         return remote(pay.at[:, columns(dst, c)], slab.at[c, dev_rows(me), :], fwd_send.at[dst, c], fwd_recv.at[me, c], dst)
@@ -97,30 +96,38 @@
     barrier = pltpu.get_barrier_semaphore()
     for dst in near:
         pl.semaphore_signal(barrier, inc=1, device_id={'group': dst}, device_id_type=MESH)
-    for dst in far + near:
-        pay_copy(dst).start()
-    for copy in own_copies:
+    for dst in far:
+        pay_copy(dst, 0).start()
+    for copy in own_copies[:2]:
         copy.start()
+    for dst in near:
+        pay_copy(dst, 0).start()
     pl.semaphore_wait(barrier, len(near))
     pl.semaphore_signal(far_ok, inc=1, device_id={'group': peer(way(1), 0)}, device_id_type=MESH)
 
+    for flip in range(CORES):
+        pay_copy(far[flip], 0).wait()
+        for i in range(WAYS):
+            hop_out(i, flip, 0).start()
+    for copy in own_copies[:2]:
+        copy.wait()
     for dst in near:
         key_copy(dst).start()
         seg_copy(dst).start()
-    for dst in far:
-        pay_copy(dst).wait()
-    for i, flip in both:
-        hop_out(i, flip, 0).start()
+    for dst in far + near:
+        pay_copy(dst, 1).start()
+    for copy in own_copies[2:]:
+        copy.start()
     pl.semaphore_wait(far_ok, 1)
     for dst in far:
         key_copy(dst).start()
         seg_copy(dst).start()
     for dst in near:
-        pay_copy(dst).wait()
+        pay_copy(dst, 0).wait()
         fwd_copy(dst, 0).start()
-
-    own_copies[0].wait()
-    own_copies[1].wait()
+    for dst in far + near:
+        pay_copy(dst, 1).wait()
+
     for src in far + near:
         arrived(keys_all.at[src], key_recv.at[src])
         arrived(segs_all.at[src], seg_recv.at[src])
@@ -285,7 +292,7 @@
                 pltpu.VMEM((CHUNKS, total, cw), jnp.bfloat16),
                 pltpu.VMEM((*hops, rows // WAYS, cw), jnp.bfloat16),
                 pltpu.VMEM((*hops, rows // WAYS, cw), jnp.bfloat16),
-                pltpu.SemaphoreType.REGULAR, dma((n,)), dma((n,)), dma((n,)), dma((n,)), dma((n,)),
+                pltpu.SemaphoreType.REGULAR, dma((n, CHUNKS)), dma((n,)), dma((n,)), dma((n,)), dma((n,)),
                 dma((n, CHUNKS)), dma((n, CHUNKS)),
                 dma(hops), dma(hops), dma(hops), dma((n, CHUNKS, WAYS)),
                 dma((n, CHUNKS, WAYS)), dma((n, CHUNKS, WAYS)), dma(hops), dma(hops), dma(hops),

time: 100 us -> 100 us (level)
  no operation moved by 1% of the time
where the time goes in v5:
time: 100 us
  Pallas kernels  98.3 us (98%)
  local copies, waits for them, and re-layouts  2.02 us (2%)
    pallas_call x1, Pallas kernels, per_device(): pl.pallas_call(functools.partial(exchange_kernel, n), out_shape=pltpu.VME...  98.3 us
    unnamed x1, local copies, waits for them, and re-layouts  2.02 us

profile of v5, /device:TPU:81, one launch (start us, length us, event | category | flops | bytes accessed | tf_op | source)
XLA Modules:
  0.0 100.3 jit_solution(14758651865200264813)
XLA Ops:
  0.0 98.3 %exchange_sums.1 = bf16[512,4096]{1,0:T(8,128)(2,1)S(1)} custom-call(f32[1,1,512]{2,1,0:T(1,128)} %bitcast.2, s32[1,1,512]{2,1,0:T(1,128)} %bitcast.3, bf16[512,4096]{1,0:T(8,128)(2,1)} %pay_ref.1), custom_call_target="tpu_custom_call" | custom-call | tf_op jit(solution)/shard_map/exchange_sums/pallas_call | solution.py:279
  98.3 2.0 %copy.5 = bf16[512,4096]{1,0:T(8,128)(2,1)} copy(bf16[512,4096]{1,0:T(8,128)(2,1)S(1)} %exchange_sums.1) | data formatting | bytes 8388608

commit v6 on v4

v6 whole, which is shorter than its diff:
```python
import functools

import jax
import jax.numpy as jnp
from jax import lax
from jax.experimental import pallas as pl
from jax.experimental.pallas import tpu as pltpu
from jax.sharding import PartitionSpec as P

MESH = pl.DeviceIdType.MESH
LANES = 128
CORES = 2
WAYS = 2
CHUNKS = 2
ROW_TILE = 64
EARLY_STEPS = 16
PARTS = 2


def exchange_kernel(n, keys_ref, segs_ref, pay_ref, out_ref, keys_all, segs_all, kcol, scol, mask, pay, slab, res,
                    relay, relay_back, far_ok, pay_sem, key_send, key_recv, seg_send, seg_recv, fwd_send, fwd_recv,
                    hop_send, hop_recv, on_send, ret_send, ret_recv, back_send, back_recv, back_on_send):
    me = lax.axis_index('group')
    rows, width = pay_ref.shape
    block = width // n
    cw = block // CHUNKS
    part = rows // PARTS
    lane_tiles = rows // LANES
    ring = n // CORES
    chip, core = lax.div(me, CORES), lax.rem(me, CORES)

    def peer(hop, flip):
        return lax.rem(chip + hop, ring) * CORES + lax.rem(core + flip, CORES)

    def way(i):
        return 1 + (ring - 2) * i

    near = [peer(way(i), flip) for flip in range(CORES) for i in range(WAYS)] + [peer(0, 1)]
    far = [peer(2, flip) for flip in range(CORES)]

    def remote(src, dst, send_sem, recv_sem, dev):
        return pltpu.make_async_remote_copy(src_ref=src, dst_ref=dst, send_sem=send_sem, recv_sem=recv_sem,
                                            device_id={'group': dev}, device_id_type=MESH)

    def columns(dev, c):
        return pl.ds(pl.multiple_of(dev * block + c * cw, LANES), cw)

    def dev_rows(dev):
        return pl.ds(pl.multiple_of(dev * rows, rows), rows)

    def part_rows(dev, i):
        return pl.ds(pl.multiple_of(dev * rows + i * part, part), part)

    def key_copy(dst):
        return remote(keys_ref.at[0], keys_all.at[me], key_send.at[dst], key_recv.at[me], dst)

    def seg_copy(dst):
        return remote(segs_ref.at[0], segs_all.at[me], seg_send.at[dst], seg_recv.at[me], dst)

    def pay_copy(dst):
        cols = pl.ds(pl.multiple_of(dst * block, LANES), block)
        return pltpu.make_async_copy(pay_ref.at[:, cols], pay.at[:, cols], pay_sem.at[dst])

    def fwd_copy(dst, c):
        return remote(pay.at[:, columns(dst, c)], slab.at[c, dev_rows(me), :], fwd_send.at[dst, c], fwd_recv.at[me, c], dst)

    def hop_out(i, c):
        return remote(pay.at[:, columns(peer(2, i), c)], relay.at[i, c], hop_send.at[i, c], hop_recv.at[i, c], peer(way(i), 0))

    def hop_on(i, c):
        origin = peer(way(1 - i), 0)
        return remote(relay.at[i, c], slab.at[c, dev_rows(origin), :], on_send.at[i, c], fwd_recv.at[origin, c], peer(way(i), i))

    def ret_copy(dst, c):
        return remote(res.at[c, dev_rows(dst), :], out_ref.at[:, columns(me, c)], ret_send.at[dst, c], ret_recv.at[me, c], dst)

    def back_out(i, c):
        return remote(res.at[c, dev_rows(peer(2, i)), :], relay_back.at[i, c], back_send.at[i, c], back_recv.at[i, c],
                      peer(way(i), 0))

    def back_on(i, c):
        origin = peer(way(1 - i), 0)
        return remote(relay_back.at[i, c], out_ref.at[:, columns(origin, c)], back_on_send.at[i, c], ret_recv.at[origin, c],
                      peer(way(i), i))

    def arrived(dst, sem):
        pltpu.make_async_copy(dst, dst, sem).wait()

    own_copies = [pltpu.make_async_copy(keys_ref.at[0], keys_all.at[me], key_recv.at[me]),
                  pltpu.make_async_copy(segs_ref.at[0], segs_all.at[me], seg_recv.at[me])]
    own_copies += [pltpu.make_async_copy(pay_ref.at[:, columns(me, c)], slab.at[c, dev_rows(me), :], fwd_recv.at[me, c])
                   for c in range(CHUNKS)]

    barrier = pltpu.get_barrier_semaphore()
    for dst in near:
        pl.semaphore_signal(barrier, inc=1, device_id={'group': dst}, device_id_type=MESH)
    for dst in far + near:
        pay_copy(dst).start()
    for copy in own_copies:
        copy.start()
    pl.semaphore_wait(barrier, len(near))
    pl.semaphore_signal(far_ok, inc=1, device_id={'group': peer(way(1), 0)}, device_id_type=MESH)

    for dst in near:
        key_copy(dst).start()
        seg_copy(dst).start()
    for dst in far:
        pay_copy(dst).wait()
    for i in range(WAYS):
        hop_out(i, 0).start()
    pl.semaphore_wait(far_ok, 1)
    for dst in far:
        key_copy(dst).start()
        seg_copy(dst).start()
    for dst in near:
        pay_copy(dst).wait()
        fwd_copy(dst, 0).start()

    own_copies[0].wait()
    own_copies[1].wait()
    for src in far + near:
        arrived(keys_all.at[src], key_recv.at[src])
        arrived(segs_all.at[src], seg_recv.at[src])

    def spread(dev, carry):
        for j in range(lane_tiles):
            lanes = slice(j * LANES, (j + 1) * LANES)
            dst = pl.ds(pl.multiple_of(dev * rows + j * LANES, LANES), LANES)
            kcol[dst, :] = jnp.broadcast_to(keys_all[dev, :, lanes], (LANES, LANES)).T
            scol[dst, :] = jnp.broadcast_to(segs_all[dev, :, lanes], (LANES, LANES)).T
        return carry

    lax.fori_loop(0, n, spread, 0)

    def build(t, carry):
        here = pl.ds(pl.multiple_of(t * ROW_TILE, ROW_TILE), ROW_TILE)
        key_r, seg_r = kcol[here, :], scol[here, :]
        last = jnp.full((ROW_TILE, LANES), -jnp.inf, jnp.float32)
        for dev in range(n):
            for j in range(lane_tiles):
                lanes = slice(j * LANES, (j + 1) * LANES)
                key_s, seg_s = keys_all[dev, :, lanes], segs_all[dev, :, lanes]
                other = jnp.logical_and(key_s < key_r, seg_s != seg_r)
                last = jnp.maximum(last, jnp.where(other, key_s, -jnp.inf))
        last = jnp.broadcast_to(jnp.max(last, axis=1, keepdims=True), (ROW_TILE, LANES))
        for dev in range(n):
            for j in range(lane_tiles):
                lanes = slice(j * LANES, (j + 1) * LANES)
                key_s = keys_all[dev, :, lanes]
                inside = jnp.logical_and(key_s <= key_r, key_s > last)
                at = slice(dev * rows + j * LANES, dev * rows + (j + 1) * LANES)
                mask[here, at] = jnp.where(inside, 1.0, 0.0).astype(jnp.bfloat16)
        return carry

    steps = n * rows // ROW_TILE
    for c in range(CHUNKS):
        lax.fori_loop(EARLY_STEPS * c, EARLY_STEPS * (c + 1) if c < CHUNKS - 1 else steps, build, 0)
        for i in range(WAYS):
            arrived(relay.at[i, c], hop_recv.at[i, c])
            hop_on(i, c).start()
        if c + 1 < CHUNKS:
            for i in range(WAYS):
                hop_out(i, c + 1).start()
            for dst in near:
                fwd_copy(dst, c + 1).start()

    def sums(dev, i, c):
        return jnp.dot(mask[part_rows(dev, i), :], slab[c], preferred_element_type=jnp.float32).astype(jnp.bfloat16)

    def near_pick(k):
        return peer(way(lax.rem(k, WAYS)), lax.div(k, WAYS))

    for c in range(CHUNKS):
        own_copies[2 + c].wait()
        for src in near + far:
            arrived(slab.at[c, dev_rows(src), :], fwd_recv.at[src, c])

        def block_step(pick, before, send, c=c):
            def step_fn(step, carry):
                k, i = lax.div(step, PARTS), lax.rem(step, PARTS)
                dev = pick(k)
                res[c, part_rows(dev, i), :] = sums(dev, i, c)

                if before is not None:
                    @pl.when(step == 0)
                    def _():
                        before.start()

                @pl.when(jnp.logical_and(i == 0, step > 0))
                def _():
                    send(k - 1).start()

                return carry
            return step_fn

        lax.fori_loop(0, WAYS * PARTS, block_step(lambda k: peer(2, k), None, lambda k: back_out(k, c)), 0)
        lax.fori_loop(0, WAYS * CORES * PARTS,
                      block_step(near_pick, back_out(WAYS - 1, c), lambda k: ret_copy(near_pick(k), c)), 0)
        lax.fori_loop(0, PARTS, block_step(lambda k: peer(0, 1), ret_copy(near[-2], c), lambda k: ret_copy(near[-1], c)), 0)

        def own_step(i, carry, c=c):
            out_ref[part_rows(0, i), columns(me, c)] = sums(me, i, c)

            @pl.when(i == 0)
            def _():
                ret_copy(near[-1], c).start()

            return carry

        lax.fori_loop(0, PARTS, own_step, 0)

    for c in range(CHUNKS):
        for i in range(WAYS):
            arrived(relay_back.at[i, c], back_recv.at[i, c])
            back_on(i, c).start()

    for dst in far + near:
        key_copy(dst).wait_send()
        seg_copy(dst).wait_send()
    for c in range(CHUNKS):
        for dst in near:
            fwd_copy(dst, c).wait_send()
            ret_copy(dst, c).wait_send()
        for i in range(WAYS):
            hop_out(i, c).wait_send()
            hop_on(i, c).wait_send()
            back_out(i, c).wait_send()
        for src in near + far:
            arrived(out_ref.at[:, columns(src, c)], ret_recv.at[src, c])
    for c in range(CHUNKS):
        for i in range(WAYS):
            back_on(i, c).wait_send()


def solution(mesh):
    n = mesh.shape['group']

    def per_device(sort_keys, seg_ids, payload):
        rows, width = payload.shape
        total = n * rows
        cw = width // n // CHUNKS
        dma = pltpu.SemaphoreType.DMA
        hops = (WAYS, CHUNKS)
        return pl.pallas_call(
            functools.partial(exchange_kernel, n),
            out_shape=pltpu.VMEM((rows, width), jnp.bfloat16),
            in_specs=[pl.BlockSpec(memory_space=pl.ANY)] * 3,
            out_specs=pl.BlockSpec(memory_space=pltpu.VMEM),
            scratch_shapes=[
                pltpu.VMEM((n, 1, rows), jnp.float32),
                pltpu.VMEM((n, 1, rows), jnp.int32),
                pltpu.VMEM((total, LANES), jnp.float32),
                pltpu.VMEM((total, LANES), jnp.int32),
                pltpu.VMEM((total, total), jnp.bfloat16),
                pltpu.VMEM((rows, width), jnp.bfloat16),
                pltpu.VMEM((CHUNKS, total, cw), jnp.bfloat16),
                pltpu.VMEM((CHUNKS, total, cw), jnp.bfloat16),
                pltpu.VMEM((*hops, rows, cw), jnp.bfloat16),
                pltpu.VMEM((*hops, rows, cw), jnp.bfloat16),
                pltpu.SemaphoreType.REGULAR, dma((n,)), dma((n,)), dma((n,)), dma((n,)), dma((n,)),
                dma((n, CHUNKS)), dma((n, CHUNKS)),
                dma(hops), dma(hops), dma(hops),
                dma((n, CHUNKS)), dma((n, CHUNKS)), dma(hops), dma(hops), dma(hops),
            ],
            compiler_params=pltpu.CompilerParams(collective_id=0, has_side_effects=True,
                                                 vmem_limit_bytes=56 * 1024 * 1024),
            name='exchange_sums',
        )(sort_keys.reshape(1, 1, rows), seg_ids.reshape(1, 1, rows), payload)

    row_spec = P(('batch', 'group'))
    mat_spec = P(('batch', 'group'), None)
    return jax.shard_map(per_device, mesh=mesh, in_specs=(row_spec, row_spec, mat_spec),
                         out_specs=mat_spec, check_vma=False)
```

time: 100 us -> 99.2 us (level)
  no operation moved by 1% of the time
where the time goes in v6:
time: 99.2 us
  Pallas kernels  97.1 us (98%)
  local copies, waits for them, and re-layouts  2.02 us (2%)
    pallas_call x1, Pallas kernels, per_device(): pl.pallas_call(functools.partial(exchange_kernel, n), out_shape=pltpu.VME...  97.1 us
    unnamed x1, local copies, waits for them, and re-layouts  2.02 us

profile of v6, /device:TPU:81, one launch (start us, length us, event | category | flops | bytes accessed | tf_op | source)
XLA Modules:
  0.0 99.2 jit_solution(4133712391652880042)
XLA Ops:
  0.0 97.1 %exchange_sums.1 = bf16[512,4096]{1,0:T(8,128)(2,1)S(1)} custom-call(f32[1,1,512]{2,1,0:T(1,128)} %bitcast.2, s32[1,1,512]{2,1,0:T(1,128)} %bitcast.3, bf16[512,4096]{1,0:T(8,128)(2,1)} %pay_ref.1), custom_call_target="tpu_custom_call" | custom-call | tf_op jit(solution)/shard_map/exchange_sums/pallas_call | solution.py:244
  97.1 2.0 %copy.5 = bf16[512,4096]{1,0:T(8,128)(2,1)} copy(bf16[512,4096]{1,0:T(8,128)(2,1)S(1)} %exchange_sums.1) | data formatting | bytes 8388608

commit v7 on v6

--- a/solution.py
+++ b/solution.py
@@ -67,6 +67,10 @@
     def hop_out(i, c):
         return remote(pay.at[:, columns(peer(2, i), c)], relay.at[i, c], hop_send.at[i, c], hop_recv.at[i, c], peer(way(i), 0))
 
+    def hop_part(i, c, piece):
+        return remote(pay.at[part_rows(0, piece), columns(peer(2, i), c)], relay.at[i, c, part_rows(0, piece), :],
+                      hop_send.at[i, c], hop_recv.at[i, c], peer(way(i), 0))
+
     def hop_on(i, c):
         origin = peer(way(1 - i), 0)
         return remote(relay.at[i, c], slab.at[c, dev_rows(origin), :], on_send.at[i, c], fwd_recv.at[origin, c], peer(way(i), i))
@@ -106,8 +110,17 @@
         seg_copy(dst).start()
     for dst in far:
         pay_copy(dst).wait()
-    for i in range(WAYS):
-        hop_out(i, 0).start()
+    @pl.when(core == 0)
+    def _():
+        for i in range(WAYS):
+            hop_out(i, 0).start()
+
+    @pl.when(core != 0)
+    def _():
+        for piece in range(PARTS):
+            for i in range(WAYS):
+                hop_part(i, 0, piece).start()
+
     pl.semaphore_wait(far_ok, 1)
     for dst in far:
         key_copy(dst).start()

time: 99.2 us -> 99.2 us (level)
  no operation moved by 1% of the time
where the time goes in v7:
time: 99.2 us
  Pallas kernels  97.1 us (98%)
  local copies, waits for them, and re-layouts  2.02 us (2%)
    pallas_call x1, Pallas kernels, per_device(): pl.pallas_call(functools.partial(exchange_kernel, n), out_shape=pltpu.VME...  97.1 us
    unnamed x1, local copies, waits for them, and re-layouts  2.02 us

profile of v7, /device:TPU:81, one launch (start us, length us, event | category | flops | bytes accessed | tf_op | source)
XLA Modules:
  0.0 99.2 jit_solution(10728678639758582802)
XLA Ops:
  0.0 97.1 %exchange_sums.1 = bf16[512,4096]{1,0:T(8,128)(2,1)S(1)} custom-call(f32[1,1,512]{2,1,0:T(1,128)} %bitcast.2, s32[1,1,512]{2,1,0:T(1,128)} %bitcast.3, bf16[512,4096]{1,0:T(8,128)(2,1)} %pay_ref.1), custom_call_target="tpu_custom_call" | custom-call | tf_op jit(solution)/shard_map/exchange_sums/pallas_call | solution.py:257
  97.1 2.0 %copy.5 = bf16[512,4096]{1,0:T(8,128)(2,1)} copy(bf16[512,4096]{1,0:T(8,128)(2,1)S(1)} %exchange_sums.1) | data formatting | bytes 8388608

commit v8 on v6

--- a/solution.py
+++ b/solution.py
@@ -57,9 +57,8 @@
     def seg_copy(dst):
         return remote(segs_ref.at[0], segs_all.at[me], seg_send.at[dst], seg_recv.at[me], dst)
 
-    def pay_copy(dst):
-        cols = pl.ds(pl.multiple_of(dst * block, LANES), block)
-        return pltpu.make_async_copy(pay_ref.at[:, cols], pay.at[:, cols], pay_sem.at[dst])
+    def pay_copy(dst, c):
+        return pltpu.make_async_copy(pay_ref.at[:, columns(dst, c)], pay.at[:, columns(dst, c)], pay_sem.at[dst, c])
 
     def fwd_copy(dst, c):
         return remote(pay.at[:, columns(dst, c)], slab.at[c, dev_rows(me), :], fwd_send.at[dst, c], fwd_recv.at[me, c], dst)
@@ -95,26 +94,27 @@
     for dst in near:
         pl.semaphore_signal(barrier, inc=1, device_id={'group': dst}, device_id_type=MESH)
     for dst in far + near:
-        pay_copy(dst).start()
-    for copy in own_copies:
-        copy.start()
+        pay_copy(dst, 0).start()
     pl.semaphore_wait(barrier, len(near))
     pl.semaphore_signal(far_ok, inc=1, device_id={'group': peer(way(1), 0)}, device_id_type=MESH)
 
     for dst in near:
         key_copy(dst).start()
         seg_copy(dst).start()
-    for dst in far:
-        pay_copy(dst).wait()
     for i in range(WAYS):
+        pay_copy(far[i], 0).wait()
         hop_out(i, 0).start()
     pl.semaphore_wait(far_ok, 1)
     for dst in far:
         key_copy(dst).start()
         seg_copy(dst).start()
     for dst in near:
-        pay_copy(dst).wait()
+        pay_copy(dst, 0).wait()
         fwd_copy(dst, 0).start()
+    for copy in own_copies:
+        copy.start()
+    for dst in far + near:
+        pay_copy(dst, 1).start()
 
     own_copies[0].wait()
     own_copies[1].wait()
@@ -159,6 +159,8 @@
             arrived(relay.at[i, c], hop_recv.at[i, c])
             hop_on(i, c).start()
         if c + 1 < CHUNKS:
+            for dst in far + near:
+                pay_copy(dst, c + 1).wait()
             for i in range(WAYS):
                 hop_out(i, c + 1).start()
             for dst in near:
@@ -257,7 +259,7 @@
                 pltpu.VMEM((CHUNKS, total, cw), jnp.bfloat16),
                 pltpu.VMEM((*hops, rows, cw), jnp.bfloat16),
                 pltpu.VMEM((*hops, rows, cw), jnp.bfloat16),
-                pltpu.SemaphoreType.REGULAR, dma((n,)), dma((n,)), dma((n,)), dma((n,)), dma((n,)),
+                pltpu.SemaphoreType.REGULAR, dma((n, CHUNKS)), dma((n,)), dma((n,)), dma((n,)), dma((n,)),
                 dma((n, CHUNKS)), dma((n, CHUNKS)),
                 dma(hops), dma(hops), dma(hops),
                 dma((n, CHUNKS)), dma((n, CHUNKS)), dma(hops), dma(hops), dma(hops),

time: 99.2 us -> 98.9 us (level)
  no operation moved by 1% of the time
where the time goes in v8:
time: 98.9 us; the launch traced here: 98.8 us
  Pallas kernels  96.8 us (98%)
  local copies, waits for them, and re-layouts  2.02 us (2%)
    pallas_call x1, Pallas kernels, per_device(): pl.pallas_call(functools.partial(exchange_kernel, n), out_shape=pltpu.VME...  96.8 us
    unnamed x1, local copies, waits for them, and re-layouts  2.02 us

profile of v8, /device:TPU:81, one launch (start us, length us, event | category | flops | bytes accessed | tf_op | source)
XLA Modules:
  0.0 98.8 jit_solution(2130250466873185224)
XLA Ops:
  0.0 96.8 %exchange_sums.1 = bf16[512,4096]{1,0:T(8,128)(2,1)S(1)} custom-call(f32[1,1,512]{2,1,0:T(1,128)} %bitcast.2, s32[1,1,512]{2,1,0:T(1,128)} %bitcast.3, bf16[512,4096]{1,0:T(8,128)(2,1)} %pay_ref.1), custom_call_target="tpu_custom_call" | custom-call | tf_op jit(solution)/shard_map/exchange_sums/pallas_call | solution.py:246
  96.8 2.0 %copy.5 = bf16[512,4096]{1,0:T(8,128)(2,1)} copy(bf16[512,4096]{1,0:T(8,128)(2,1)S(1)} %exchange_sums.1) | data formatting | bytes 8388608

commit v9 on v8

v9 whole, which is shorter than its diff:
```python
import functools

import jax
import jax.numpy as jnp
from jax import lax
from jax.experimental import pallas as pl
from jax.experimental.pallas import tpu as pltpu
from jax.sharding import PartitionSpec as P

MESH = pl.DeviceIdType.MESH
LANES = 128
CORES = 2
WAYS = 2
CHUNKS = 2
ROW_TILE = 64
EARLY_STEPS = 32
PARTS = 2


def exchange_kernel(n, keys_ref, segs_ref, pay_ref, out_ref, keys_all, segs_all, kcol, scol, mask, pay, slab, res,
                    relay, relay_back, far_ok, pay_sem, key_send, key_recv, seg_send, seg_recv, fwd_send, fwd_recv,
                    hop_send, hop_recv, on_send, ret_send, ret_recv, back_send, back_recv, back_on_send):
    me = lax.axis_index('group')
    rows, width = pay_ref.shape
    block = width // n
    cw = block // CHUNKS
    part = rows // PARTS
    lane_tiles = rows // LANES
    ring = n // CORES
    chip, core = lax.div(me, CORES), lax.rem(me, CORES)

    def peer(hop, flip):
        return lax.rem(chip + hop, ring) * CORES + lax.rem(core + flip, CORES)

    def way(i):
        return 1 + (ring - 2) * i

    near = [peer(way(i), flip) for flip in range(CORES) for i in range(WAYS)] + [peer(0, 1)]
    far = [peer(2, flip) for flip in range(CORES)]

    def remote(src, dst, send_sem, recv_sem, dev):
        return pltpu.make_async_remote_copy(src_ref=src, dst_ref=dst, send_sem=send_sem, recv_sem=recv_sem,
                                            device_id={'group': dev}, device_id_type=MESH)

    def columns(dev, c):
        return pl.ds(pl.multiple_of(dev * block + c * cw, LANES), cw)

    def block_cols(dev):
        return pl.ds(pl.multiple_of(dev * block, LANES), block)

    def chunk(c):
        return pl.ds(c * cw, cw)

    def dev_rows(dev):
        return pl.ds(pl.multiple_of(dev * rows, rows), rows)

    def part_rows(dev, i):
        return pl.ds(pl.multiple_of(dev * rows + i * part, part), part)

    def key_copy(dst):
        return remote(keys_ref.at[0], keys_all.at[me], key_send.at[dst], key_recv.at[me], dst)

    def seg_copy(dst):
        return remote(segs_ref.at[0], segs_all.at[me], seg_send.at[dst], seg_recv.at[me], dst)

    def pay_copy(dst, c):
        return pltpu.make_async_copy(pay_ref.at[:, columns(dst, c)], pay.at[:, columns(dst, c)], pay_sem.at[dst, c])

    def fwd_copy(dst, c):
        return remote(pay.at[:, columns(dst, c)], slab.at[dev_rows(me), chunk(c)], fwd_send.at[dst, c], fwd_recv.at[me, c], dst)

    def hop_out(i):
        return remote(pay.at[:, block_cols(peer(2, i))], relay.at[i], hop_send.at[i], hop_recv.at[i], peer(way(i), 0))

    def hop_on(i):
        origin = peer(way(1 - i), 0)
        return remote(relay.at[i], slab.at[dev_rows(origin), :], on_send.at[i], fwd_recv.at[origin, 0], peer(way(i), i))

    def ret_copy(dst, c):
        return remote(res.at[dev_rows(dst), chunk(c)], out_ref.at[:, columns(me, c)], ret_send.at[dst, c], ret_recv.at[me], dst)

    def ret_whole(dst):
        return remote(res.at[dev_rows(dst), :], out_ref.at[:, block_cols(me)], ret_send.at[dst, 0], ret_recv.at[me], dst)

    def back_out(i, c):
        return remote(res.at[dev_rows(peer(2, i)), chunk(c)], relay_back.at[i, :, chunk(c)], back_send.at[i, c],
                      back_recv.at[i], peer(way(i), 0))

    def back_on(i):
        origin = peer(way(1 - i), 0)
        return remote(relay_back.at[i], out_ref.at[:, block_cols(origin)], back_on_send.at[i], ret_recv.at[origin],
                      peer(way(i), i))

    def arrived(dst, sem):
        pltpu.make_async_copy(dst, dst, sem).wait()

    own_copies = [pltpu.make_async_copy(keys_ref.at[0], keys_all.at[me], key_recv.at[me]),
                  pltpu.make_async_copy(segs_ref.at[0], segs_all.at[me], seg_recv.at[me])]
    own_copies += [pltpu.make_async_copy(pay_ref.at[:, columns(me, c)], slab.at[dev_rows(me), chunk(c)], fwd_recv.at[me, c])
                   for c in range(CHUNKS)]

    barrier = pltpu.get_barrier_semaphore()
    for dst in near:
        pl.semaphore_signal(barrier, inc=1, device_id={'group': dst}, device_id_type=MESH)
    for dst in far:
        for c in range(CHUNKS):
            pay_copy(dst, c).start()
    for dst in near:
        pay_copy(dst, 0).start()
    pl.semaphore_wait(barrier, len(near))
    pl.semaphore_signal(far_ok, inc=1, device_id={'group': peer(way(1), 0)}, device_id_type=MESH)

    for dst in near:
        key_copy(dst).start()
        seg_copy(dst).start()
    for i in range(WAYS):
        for c in range(CHUNKS):
            pay_copy(far[i], c).wait()
        hop_out(i).start()
    pl.semaphore_wait(far_ok, 1)
    for dst in far:
        key_copy(dst).start()
        seg_copy(dst).start()
    for dst in near:
        pay_copy(dst, 0).wait()
        fwd_copy(dst, 0).start()
    for copy in own_copies:
        copy.start()
    for dst in near:
        pay_copy(dst, 1).start()

    own_copies[0].wait()
    own_copies[1].wait()
    for src in far + near:
        arrived(keys_all.at[src], key_recv.at[src])
        arrived(segs_all.at[src], seg_recv.at[src])

    def spread(dev, carry):
        for j in range(lane_tiles):
            lanes = slice(j * LANES, (j + 1) * LANES)
            dst = pl.ds(pl.multiple_of(dev * rows + j * LANES, LANES), LANES)
            kcol[dst, :] = jnp.broadcast_to(keys_all[dev, :, lanes], (LANES, LANES)).T
            scol[dst, :] = jnp.broadcast_to(segs_all[dev, :, lanes], (LANES, LANES)).T
        return carry

    lax.fori_loop(0, n, spread, 0)

    def build(t, carry):
        here = pl.ds(pl.multiple_of(t * ROW_TILE, ROW_TILE), ROW_TILE)
        key_r, seg_r = kcol[here, :], scol[here, :]
        last = jnp.full((ROW_TILE, LANES), -jnp.inf, jnp.float32)
        for dev in range(n):
            for j in range(lane_tiles):
                lanes = slice(j * LANES, (j + 1) * LANES)
                key_s, seg_s = keys_all[dev, :, lanes], segs_all[dev, :, lanes]
                other = jnp.logical_and(key_s < key_r, seg_s != seg_r)
                last = jnp.maximum(last, jnp.where(other, key_s, -jnp.inf))
        last = jnp.broadcast_to(jnp.max(last, axis=1, keepdims=True), (ROW_TILE, LANES))
        for dev in range(n):
            for j in range(lane_tiles):
                lanes = slice(j * LANES, (j + 1) * LANES)
                key_s = keys_all[dev, :, lanes]
                inside = jnp.logical_and(key_s <= key_r, key_s > last)
                at = slice(dev * rows + j * LANES, dev * rows + (j + 1) * LANES)
                mask[here, at] = jnp.where(inside, 1.0, 0.0).astype(jnp.bfloat16)
        return carry

    lax.fori_loop(0, EARLY_STEPS, build, 0)
    for i in range(WAYS):
        arrived(relay.at[i], hop_recv.at[i])
        hop_on(i).start()
    for dst in near:
        pay_copy(dst, 1).wait()
        fwd_copy(dst, 1).start()
    lax.fori_loop(EARLY_STEPS, n * rows // ROW_TILE, build, 0)

    def sums(dev, i, c):
        return jnp.dot(mask[part_rows(dev, i), :], slab[:, chunk(c)], preferred_element_type=jnp.float32).astype(jnp.bfloat16)

    def blocks(count, pick, c, before, send):
        def step_fn(step, carry):
            k, i = lax.div(step, PARTS), lax.rem(step, PARTS)
            dev = pick(k)
            res[part_rows(dev, i), chunk(c)] = sums(dev, i, c)

            if before is not None:
                @pl.when(step == 0)
                def _():
                    before.start()

            if send is not None:
                @pl.when(jnp.logical_and(i == 0, step > 0))
                def _():
                    send(k - 1).start()

            return carry

        lax.fori_loop(0, count * PARTS, step_fn, 0)

    def own_block(c, before):
        def step_fn(i, carry):
            out_ref[part_rows(0, i), columns(me, c)] = sums(me, i, c)

            if before is not None:
                @pl.when(i == 0)
                def _():
                    before.start()

            return carry

        lax.fori_loop(0, PARTS, step_fn, 0)

    def far_dev(k):
        return peer(2, k)

    def near_a(k):
        return peer(way(k), 0)

    def near_b(k):
        return peer(way(k), 1)

    def chip_dev(k):
        return peer(0, 1)

    own_copies[2].wait()
    for src in near:
        arrived(slab.at[dev_rows(src), chunk(0)], fwd_recv.at[src, 0])
    for src in far:
        arrived(slab.at[dev_rows(src), :], fwd_recv.at[src, 0])
    blocks(WAYS, far_dev, 0, None, lambda k: back_out(k, 0))
    blocks(WAYS, near_a, 0, back_out(WAYS - 1, 0), lambda k: ret_copy(near_a(k), 0))
    blocks(WAYS, near_b, 0, ret_copy(near_a(WAYS - 1), 0), None)
    blocks(1, chip_dev, 0, None, None)
    own_block(0, None)
    own_copies[3].wait()
    for src in near:
        arrived(slab.at[dev_rows(src), chunk(1)], fwd_recv.at[src, 1])
    blocks(WAYS, near_a, 1, None, lambda k: ret_copy(near_a(k), 1))
    blocks(WAYS, far_dev, 1, ret_copy(near_a(WAYS - 1), 1), lambda k: back_out(k, 1))
    blocks(WAYS, near_b, 1, back_out(WAYS - 1, 1), lambda k: ret_whole(near_b(k)))
    blocks(1, chip_dev, 1, ret_whole(near_b(WAYS - 1)), None)
    own_block(1, ret_whole(peer(0, 1)))

    for i in range(WAYS):
        arrived(relay_back.at[i], back_recv.at[i])
        back_on(i).start()

    for dst in far + near:
        key_copy(dst).wait_send()
        seg_copy(dst).wait_send()
    for c in range(CHUNKS):
        for dst in near:
            fwd_copy(dst, c).wait_send()
    for i in range(WAYS):
        hop_out(i).wait_send()
        hop_on(i).wait_send()
        for c in range(CHUNKS):
            back_out(i, c).wait_send()
            ret_copy(near_a(i), c).wait_send()
        ret_whole(near_b(i)).wait_send()
    ret_whole(peer(0, 1)).wait_send()
    for src in near + far:
        arrived(out_ref.at[:, block_cols(src)], ret_recv.at[src])
    for i in range(WAYS):
        back_on(i).wait_send()


def solution(mesh):
    n = mesh.shape['group']

    def per_device(sort_keys, seg_ids, payload):
        rows, width = payload.shape
        total = n * rows
        dma = pltpu.SemaphoreType.DMA
        block = width // n
        return pl.pallas_call(
            functools.partial(exchange_kernel, n),
            out_shape=pltpu.VMEM((rows, width), jnp.bfloat16),
            in_specs=[pl.BlockSpec(memory_space=pl.ANY)] * 3,
            out_specs=pl.BlockSpec(memory_space=pltpu.VMEM),
            scratch_shapes=[
                pltpu.VMEM((n, 1, rows), jnp.float32),
                pltpu.VMEM((n, 1, rows), jnp.int32),
                pltpu.VMEM((total, LANES), jnp.float32),
                pltpu.VMEM((total, LANES), jnp.int32),
                pltpu.VMEM((total, total), jnp.bfloat16),
                pltpu.VMEM((rows, width), jnp.bfloat16),
                pltpu.VMEM((total, block), jnp.bfloat16),
                pltpu.VMEM((total, block), jnp.bfloat16),
                pltpu.VMEM((WAYS, rows, block), jnp.bfloat16),
                pltpu.VMEM((WAYS, rows, block), jnp.bfloat16),
                pltpu.SemaphoreType.REGULAR, dma((n, CHUNKS)), dma((n,)), dma((n,)), dma((n,)), dma((n,)),
                dma((n, CHUNKS)), dma((n, CHUNKS)), dma((WAYS,)), dma((WAYS,)), dma((WAYS,)),
                dma((n, CHUNKS)), dma((n,)), dma((WAYS, CHUNKS)), dma((WAYS,)), dma((WAYS,)),
            ],
            compiler_params=pltpu.CompilerParams(collective_id=0, has_side_effects=True,
                                                 vmem_limit_bytes=56 * 1024 * 1024),
            name='exchange_sums',
        )(sort_keys.reshape(1, 1, rows), seg_ids.reshape(1, 1, rows), payload)

    row_spec = P(('batch', 'group'))
    mat_spec = P(('batch', 'group'), None)
    return jax.shard_map(per_device, mesh=mesh, in_specs=(row_spec, row_spec, mat_spec),
                         out_specs=mat_spec, check_vma=False)
```

time: 98.9 us -> 105 us (1.062)
  Pallas kernels: 96.8 us -> 103 us
    pallas_call x1, Pallas kernels: 96.8 us -> 103 us  [per_device(): pl.pallas_call(functools.partial(exchange_kernel, n), out_shape=pltpu.VME...]
where the time goes in v9:
time: 105 us
  Pallas kernels  103 us (98%)
  local copies, waits for them, and re-layouts  2.02 us (2%)
    pallas_call x1, Pallas kernels, per_device(): pl.pallas_call(functools.partial(exchange_kernel, n), out_shape=pltpu.VME...  103 us

profile of v9, /device:TPU:81, one launch (start us, length us, event | category | flops | bytes accessed | tf_op | source)
XLA Modules:
  0.0 104.6 jit_solution(736443038409321659)
XLA Ops:
  0.0 102.6 %exchange_sums.1 = bf16[512,4096]{1,0:T(8,128)(2,1)S(1)} custom-call(f32[1,1,512]{2,1,0:T(1,128)} %bitcast.2, s32[1,1,512]{2,1,0:T(1,128)} %bitcast.3, bf16[512,4096]{1,0:T(8,128)(2,1)} %pay_ref.1), custom_call_target="tpu_custom_call" | custom-call | tf_op jit(solution)/shard_map/exchange_sums/pallas_call | solution.py:276
  102.6 2.0 %copy.5 = bf16[512,4096]{1,0:T(8,128)(2,1)} copy(bf16[512,4096]{1,0:T(8,128)(2,1)S(1)} %exchange_sums.1) | data formatting | bytes 8388608

commit v10 on v8

--- a/solution.py
+++ b/solution.py
@@ -13,13 +13,13 @@
 WAYS = 2
 CHUNKS = 2
 ROW_TILE = 64
-EARLY_STEPS = 16
+EARLY_STEPS = 38
 PARTS = 2
 
 
 def exchange_kernel(n, keys_ref, segs_ref, pay_ref, out_ref, keys_all, segs_all, kcol, scol, mask, pay, slab, res,
-                    relay, relay_back, far_ok, pay_sem, key_send, key_recv, seg_send, seg_recv, fwd_send, fwd_recv,
-                    hop_send, hop_recv, on_send, ret_send, ret_recv, back_send, back_recv, back_on_send):
+                    far_ok, pay_sem, key_send, key_recv, seg_send, seg_recv, fwd_send, fwd_recv,
+                    ret_send, ret_recv):
     me = lax.axis_index('group')
     rows, width = pay_ref.shape
     block = width // n
@@ -63,24 +63,8 @@
     def fwd_copy(dst, c):
         return remote(pay.at[:, columns(dst, c)], slab.at[c, dev_rows(me), :], fwd_send.at[dst, c], fwd_recv.at[me, c], dst)
 
-    def hop_out(i, c):
-        return remote(pay.at[:, columns(peer(2, i), c)], relay.at[i, c], hop_send.at[i, c], hop_recv.at[i, c], peer(way(i), 0))
-
-    def hop_on(i, c):
-        origin = peer(way(1 - i), 0)
-        return remote(relay.at[i, c], slab.at[c, dev_rows(origin), :], on_send.at[i, c], fwd_recv.at[origin, c], peer(way(i), i))
-
     def ret_copy(dst, c):
         return remote(res.at[c, dev_rows(dst), :], out_ref.at[:, columns(me, c)], ret_send.at[dst, c], ret_recv.at[me, c], dst)
-
-    def back_out(i, c):
-        return remote(res.at[c, dev_rows(peer(2, i)), :], relay_back.at[i, c], back_send.at[i, c], back_recv.at[i, c],
-                      peer(way(i), 0))
-
-    def back_on(i, c):
-        origin = peer(way(1 - i), 0)
-        return remote(relay_back.at[i, c], out_ref.at[:, columns(origin, c)], back_on_send.at[i, c], ret_recv.at[origin, c],
-                      peer(way(i), i))
 
     def arrived(dst, sem):
         pltpu.make_async_copy(dst, dst, sem).wait()
@@ -93,7 +77,7 @@
     barrier = pltpu.get_barrier_semaphore()
     for dst in near:
         pl.semaphore_signal(barrier, inc=1, device_id={'group': dst}, device_id_type=MESH)
-    for dst in far + near:
+    for dst in near + far:
         pay_copy(dst, 0).start()
     pl.semaphore_wait(barrier, len(near))
     pl.semaphore_signal(far_ok, inc=1, device_id={'group': peer(way(1), 0)}, device_id_type=MESH)
@@ -101,14 +85,14 @@
     for dst in near:
         key_copy(dst).start()
         seg_copy(dst).start()
-    for i in range(WAYS):
-        pay_copy(far[i], 0).wait()
-        hop_out(i, 0).start()
+    for dst in near:
+        pay_copy(dst, 0).wait()
+        fwd_copy(dst, 0).start()
     pl.semaphore_wait(far_ok, 1)
     for dst in far:
         key_copy(dst).start()
         seg_copy(dst).start()
-    for dst in near:
+    for dst in far:
         pay_copy(dst, 0).wait()
         fwd_copy(dst, 0).start()
     for copy in own_copies:
@@ -155,15 +139,9 @@
     steps = n * rows // ROW_TILE
     for c in range(CHUNKS):
         lax.fori_loop(EARLY_STEPS * c, EARLY_STEPS * (c + 1) if c < CHUNKS - 1 else steps, build, 0)
-        for i in range(WAYS):
-            arrived(relay.at[i, c], hop_recv.at[i, c])
-            hop_on(i, c).start()
         if c + 1 < CHUNKS:
             for dst in far + near:
                 pay_copy(dst, c + 1).wait()
-            for i in range(WAYS):
-                hop_out(i, c + 1).start()
-            for dst in near:
                 fwd_copy(dst, c + 1).start()
 
     def sums(dev, i, c):
@@ -195,9 +173,9 @@
                 return carry
             return step_fn
 
-        lax.fori_loop(0, WAYS * PARTS, block_step(lambda k: peer(2, k), None, lambda k: back_out(k, c)), 0)
+        lax.fori_loop(0, WAYS * PARTS, block_step(lambda k: peer(2, k), None, lambda k: ret_copy(peer(2, k), c)), 0)
         lax.fori_loop(0, WAYS * CORES * PARTS,
-                      block_step(near_pick, back_out(WAYS - 1, c), lambda k: ret_copy(near_pick(k), c)), 0)
+                      block_step(near_pick, ret_copy(far[-1], c), lambda k: ret_copy(near_pick(k), c)), 0)
         lax.fori_loop(0, PARTS, block_step(lambda k: peer(0, 1), ret_copy(near[-2], c), lambda k: ret_copy(near[-1], c)), 0)
 
         def own_step(i, carry, c=c):
@@ -210,28 +188,16 @@
             return carry
 
         lax.fori_loop(0, PARTS, own_step, 0)
-
-    for c in range(CHUNKS):
-        for i in range(WAYS):
-            arrived(relay_back.at[i, c], back_recv.at[i, c])
-            back_on(i, c).start()
 
     for dst in far + near:
         key_copy(dst).wait_send()
         seg_copy(dst).wait_send()
     for c in range(CHUNKS):
-        for dst in near:
+        for dst in near + far:
             fwd_copy(dst, c).wait_send()
             ret_copy(dst, c).wait_send()
-        for i in range(WAYS):
-            hop_out(i, c).wait_send()
-            hop_on(i, c).wait_send()
-            back_out(i, c).wait_send()
         for src in near + far:
             arrived(out_ref.at[:, columns(src, c)], ret_recv.at[src, c])
-    for c in range(CHUNKS):
-        for i in range(WAYS):
-            back_on(i, c).wait_send()
 
 
 def solution(mesh):
@@ -242,7 +208,6 @@
         total = n * rows
         cw = width // n // CHUNKS
         dma = pltpu.SemaphoreType.DMA
-        hops = (WAYS, CHUNKS)
         return pl.pallas_call(
             functools.partial(exchange_kernel, n),
             out_shape=pltpu.VMEM((rows, width), jnp.bfloat16),
@@ -257,12 +222,9 @@
                 pltpu.VMEM((rows, width), jnp.bfloat16),
                 pltpu.VMEM((CHUNKS, total, cw), jnp.bfloat16),
                 pltpu.VMEM((CHUNKS, total, cw), jnp.bfloat16),
-                pltpu.VMEM((*hops, rows, cw), jnp.bfloat16),
-                pltpu.VMEM((*hops, rows, cw), jnp.bfloat16),
                 pltpu.SemaphoreType.REGULAR, dma((n, CHUNKS)), dma((n,)), dma((n,)), dma((n,)), dma((n,)),
                 dma((n, CHUNKS)), dma((n, CHUNKS)),
-                dma(hops), dma(hops), dma(hops),
-                dma((n, CHUNKS)), dma((n, CHUNKS)), dma(hops), dma(hops), dma(hops),
+                dma((n, CHUNKS)), dma((n, CHUNKS)),
             ],
             compiler_params=pltpu.CompilerParams(collective_id=0, has_side_effects=True,
                                                  vmem_limit_bytes=56 * 1024 * 1024),

time: 98.9 us -> 107 us (1.082)
  Pallas kernels: 96.8 us -> 105 us
    pallas_call x1, Pallas kernels: 96.8 us -> 105 us  [per_device(): pl.pallas_call(functools.partial(exchange_kernel, n), out_shape=pltpu.VME...]
where the time goes in v10:
time: 107 us
  Pallas kernels  105 us (98%)
  local copies, waits for them, and re-layouts  2.02 us (2%)
    pallas_call x1, Pallas kernels, per_device(): pl.pallas_call(functools.partial(exchange_kernel, n), out_shape=pltpu.VME...  105 us

profile of v10, /device:TPU:81, one launch (start us, length us, event | category | flops | bytes accessed | tf_op | source)
XLA Modules:
  0.0 106.9 jit_solution(14868974906526881195)
XLA Ops:
  0.0 104.9 %exchange_sums.1 = bf16[512,4096]{1,0:T(8,128)(2,1)S(1)} custom-call(f32[1,1,512]{2,1,0:T(1,128)} %bitcast.2, s32[1,1,512]{2,1,0:T(1,128)} %bitcast.3, bf16[512,4096]{1,0:T(8,128)(2,1)} %pay_ref.1), custom_call_target="tpu_custom_call" | custom-call | tf_op jit(solution)/shard_map/exchange_sums/pallas_call | solution.py:211
  104.9 2.0 %copy.5 = bf16[512,4096]{1,0:T(8,128)(2,1)} copy(bf16[512,4096]{1,0:T(8,128)(2,1)S(1)} %exchange_sums.1) | data formatting | bytes 8388608

commit v11 on v8

--- a/solution.py
+++ b/solution.py
@@ -13,7 +13,7 @@
 WAYS = 2
 CHUNKS = 2
 ROW_TILE = 64
-EARLY_STEPS = 16
+EARLY_STEPS = 8
 PARTS = 2
 
 

time: 98.9 us -> 98.9 us (level)
  no operation moved by 1% of the time
where the time goes in v11:
time: 98.9 us; the launch traced here: 98.7 us
  Pallas kernels  96.7 us (98%)
  local copies, waits for them, and re-layouts  2.02 us (2%)
    pallas_call x1, Pallas kernels, per_device(): pl.pallas_call(functools.partial(exchange_kernel, n), out_shape=pltpu.VME...  96.7 us
    unnamed x1, local copies, waits for them, and re-layouts  2.02 us

profile of v11, /device:TPU:81, one launch (start us, length us, event | category | flops | bytes accessed | tf_op | source)
XLA Modules:
  0.0 98.7 jit_solution(10496680266522104053)
XLA Ops:
  0.0 96.7 %exchange_sums.1 = bf16[512,4096]{1,0:T(8,128)(2,1)S(1)} custom-call(f32[1,1,512]{2,1,0:T(1,128)} %bitcast.2, s32[1,1,512]{2,1,0:T(1,128)} %bitcast.3, bf16[512,4096]{1,0:T(8,128)(2,1)} %pay_ref.1), custom_call_target="tpu_custom_call" | custom-call | tf_op jit(solution)/shard_map/exchange_sums/pallas_call | solution.py:246
  96.7 2.0 %copy.5 = bf16[512,4096]{1,0:T(8,128)(2,1)} copy(bf16[512,4096]{1,0:T(8,128)(2,1)S(1)} %exchange_sums.1) | data formatting | bytes 8388608

commit v12 on v9

--- a/solution.py
+++ b/solution.py
@@ -13,7 +13,7 @@
 WAYS = 2
 CHUNKS = 2
 ROW_TILE = 64
-EARLY_STEPS = 32
+EARLY_STEPS = 8
 PARTS = 2
 
 

time: 105 us -> 98.7 us (0.940)
  Pallas kernels: 103 us -> 96.6 us
    pallas_call x1, Pallas kernels: 103 us -> 96.6 us  [per_device(): pl.pallas_call(functools.partial(exchange_kernel, n), out_shape=pltpu.VME...]
where the time goes in v12:
time: 98.7 us; the launch traced here: 98.6 us
  Pallas kernels  96.6 us (98%)
  local copies, waits for them, and re-layouts  2.02 us (2%)
    pallas_call x1, Pallas kernels, per_device(): pl.pallas_call(functools.partial(exchange_kernel, n), out_shape=pltpu.VME...  96.6 us
    unnamed x1, local copies, waits for them, and re-layouts  2.02 us

profile of v12, /device:TPU:81, one launch (start us, length us, event | category | flops | bytes accessed | tf_op | source)
XLA Modules:
  0.0 98.6 jit_solution(2309908678136768181)
XLA Ops:
  0.0 96.6 %exchange_sums.1 = bf16[512,4096]{1,0:T(8,128)(2,1)S(1)} custom-call(f32[1,1,512]{2,1,0:T(1,128)} %bitcast.2, s32[1,1,512]{2,1,0:T(1,128)} %bitcast.3, bf16[512,4096]{1,0:T(8,128)(2,1)} %pay_ref.1), custom_call_target="tpu_custom_call" | custom-call | tf_op jit(solution)/shard_map/exchange_sums/pallas_call | solution.py:276
  96.6 2.0 %copy.5 = bf16[512,4096]{1,0:T(8,128)(2,1)} copy(bf16[512,4096]{1,0:T(8,128)(2,1)S(1)} %exchange_sums.1) | data formatting | bytes 8388608

commit v13 on v12

--- a/solution.py
+++ b/solution.py
@@ -37,6 +37,7 @@
 
     near = [peer(way(i), flip) for flip in range(CORES) for i in range(WAYS)] + [peer(0, 1)]
     far = [peer(2, flip) for flip in range(CORES)]
+    same, other = near[:WAYS], near[WAYS:]
 
     def remote(src, dst, send_sem, recv_sem, dev):
         return pltpu.make_async_remote_copy(src_ref=src, dst_ref=dst, send_sem=send_sem, recv_sem=recv_sem,
@@ -68,6 +69,9 @@
 
     def fwd_copy(dst, c):
         return remote(pay.at[:, columns(dst, c)], slab.at[dev_rows(me), chunk(c)], fwd_send.at[dst, c], fwd_recv.at[me, c], dst)
+
+    def fwd_whole(dst):
+        return remote(pay.at[:, block_cols(dst)], slab.at[dev_rows(me), :], fwd_send.at[dst, 0], fwd_recv.at[me, 0], dst)
 
     def hop_out(i):
         return remote(pay.at[:, block_cols(peer(2, i))], relay.at[i], hop_send.at[i], hop_recv.at[i], peer(way(i), 0))
@@ -105,8 +109,6 @@
     for dst in far:
         for c in range(CHUNKS):
             pay_copy(dst, c).start()
-    for dst in near:
-        pay_copy(dst, 0).start()
     pl.semaphore_wait(barrier, len(near))
     pl.semaphore_signal(far_ok, inc=1, device_id={'group': peer(way(1), 0)}, device_id_type=MESH)
 
@@ -117,17 +119,25 @@
         for c in range(CHUNKS):
             pay_copy(far[i], c).wait()
         hop_out(i).start()
+    for dst in same:
+        for c in range(CHUNKS):
+            pay_copy(dst, c).start()
+    for c in range(CHUNKS):
+        for dst in other:
+            pay_copy(dst, c).start()
+    for copy in own_copies:
+        copy.start()
     pl.semaphore_wait(far_ok, 1)
     for dst in far:
         key_copy(dst).start()
         seg_copy(dst).start()
-    for dst in near:
+    for dst in same:
+        for c in range(CHUNKS):
+            pay_copy(dst, c).wait()
+        fwd_whole(dst).start()
+    for dst in other:
         pay_copy(dst, 0).wait()
         fwd_copy(dst, 0).start()
-    for copy in own_copies:
-        copy.start()
-    for dst in near:
-        pay_copy(dst, 1).start()
 
     own_copies[0].wait()
     own_copies[1].wait()
@@ -169,7 +179,7 @@
     for i in range(WAYS):
         arrived(relay.at[i], hop_recv.at[i])
         hop_on(i).start()
-    for dst in near:
+    for dst in other:
         pay_copy(dst, 1).wait()
         fwd_copy(dst, 1).start()
     lax.fori_loop(EARLY_STEPS, n * rows // ROW_TILE, build, 0)
@@ -223,9 +233,9 @@
         return peer(0, 1)
 
     own_copies[2].wait()
-    for src in near:
+    for src in other:
         arrived(slab.at[dev_rows(src), chunk(0)], fwd_recv.at[src, 0])
-    for src in far:
+    for src in same + far:
         arrived(slab.at[dev_rows(src), :], fwd_recv.at[src, 0])
     blocks(WAYS, far_dev, 0, None, lambda k: back_out(k, 0))
     blocks(WAYS, near_a, 0, back_out(WAYS - 1, 0), lambda k: ret_copy(near_a(k), 0))
@@ -233,7 +243,7 @@
     blocks(1, chip_dev, 0, None, None)
     own_block(0, None)
     own_copies[3].wait()
-    for src in near:
+    for src in other:
         arrived(slab.at[dev_rows(src), chunk(1)], fwd_recv.at[src, 1])
     blocks(WAYS, near_a, 1, None, lambda k: ret_copy(near_a(k), 1))
     blocks(WAYS, far_dev, 1, ret_copy(near_a(WAYS - 1), 1), lambda k: back_out(k, 1))
@@ -248,8 +258,10 @@
     for dst in far + near:
         key_copy(dst).wait_send()
         seg_copy(dst).wait_send()
-    for c in range(CHUNKS):
-        for dst in near:
+    for dst in same:
+        fwd_whole(dst).wait_send()
+    for dst in other:
+        for c in range(CHUNKS):
             fwd_copy(dst, c).wait_send()
     for i in range(WAYS):
         hop_out(i).wait_send()

time: 98.7 us -> 99.5 us (level)
  no operation moved by 1% of the time
where the time goes in v13:
time: 99.5 us; the launch traced here: 99.4 us
  Pallas kernels  97.4 us (98%)
  local copies, waits for them, and re-layouts  2.02 us (2%)
    pallas_call x1, Pallas kernels, per_device(): pl.pallas_call(functools.partial(exchange_kernel, n), out_shape=pltpu.VME...  97.4 us
    unnamed x1, local copies, waits for them, and re-layouts  2.02 us

profile of v13, /device:TPU:81, one launch (start us, length us, event | category | flops | bytes accessed | tf_op | source)
XLA Modules:
  0.0 99.4 jit_solution(9347744189922532052)
XLA Ops:
  0.0 97.4 %exchange_sums.1 = bf16[512,4096]{1,0:T(8,128)(2,1)S(1)} custom-call(f32[1,1,512]{2,1,0:T(1,128)} %bitcast.2, s32[1,1,512]{2,1,0:T(1,128)} %bitcast.3, bf16[512,4096]{1,0:T(8,128)(2,1)} %pay_ref.1), custom_call_target="tpu_custom_call" | custom-call | tf_op jit(solution)/shard_map/exchange_sums/pallas_call | solution.py:288
  97.4 2.0 %copy.5 = bf16[512,4096]{1,0:T(8,128)(2,1)} copy(bf16[512,4096]{1,0:T(8,128)(2,1)S(1)} %exchange_sums.1) | data formatting | bytes 8388608

commit v14 on v12

--- a/solution.py
+++ b/solution.py
@@ -105,8 +105,6 @@
     for dst in far:
         for c in range(CHUNKS):
             pay_copy(dst, c).start()
-    for dst in near:
-        pay_copy(dst, 0).start()
     pl.semaphore_wait(barrier, len(near))
     pl.semaphore_signal(far_ok, inc=1, device_id={'group': peer(way(1), 0)}, device_id_type=MESH)
 
@@ -117,6 +115,8 @@
         for c in range(CHUNKS):
             pay_copy(far[i], c).wait()
         hop_out(i).start()
+    for dst in near:
+        pay_copy(dst, 0).start()
     pl.semaphore_wait(far_ok, 1)
     for dst in far:
         key_copy(dst).start()

time: 98.7 us -> 98.7 us (level)
  no operation moved by 1% of the time
where the time goes in v14:
time: 98.7 us; the launch traced here: 98.6 us
  Pallas kernels  96.6 us (98%)
  local copies, waits for them, and re-layouts  2.02 us (2%)
    pallas_call x1, Pallas kernels, per_device(): pl.pallas_call(functools.partial(exchange_kernel, n), out_shape=pltpu.VME...  96.6 us
    unnamed x1, local copies, waits for them, and re-layouts  2.02 us

profile of v14, /device:TPU:81, one launch (start us, length us, event | category | flops | bytes accessed | tf_op | source)
XLA Modules:
  0.0 98.6 jit_solution(3174739871235443303)
XLA Ops:
  0.0 96.6 %exchange_sums.1 = bf16[512,4096]{1,0:T(8,128)(2,1)S(1)} custom-call(f32[1,1,512]{2,1,0:T(1,128)} %bitcast.2, s32[1,1,512]{2,1,0:T(1,128)} %bitcast.3, bf16[512,4096]{1,0:T(8,128)(2,1)} %pay_ref.1), custom_call_target="tpu_custom_call" | custom-call | tf_op jit(solution)/shard_map/exchange_sums/pallas_call | solution.py:276
  96.6 2.0 %copy.5 = bf16[512,4096]{1,0:T(8,128)(2,1)} copy(bf16[512,4096]{1,0:T(8,128)(2,1)S(1)} %exchange_sums.1) | data formatting | bytes 8388608

commit v15 on v12

--- a/solution.py
+++ b/solution.py
@@ -235,9 +235,9 @@
     own_copies[3].wait()
     for src in near:
         arrived(slab.at[dev_rows(src), chunk(1)], fwd_recv.at[src, 1])
-    blocks(WAYS, near_a, 1, None, lambda k: ret_copy(near_a(k), 1))
-    blocks(WAYS, far_dev, 1, ret_copy(near_a(WAYS - 1), 1), lambda k: back_out(k, 1))
-    blocks(WAYS, near_b, 1, back_out(WAYS - 1, 1), lambda k: ret_whole(near_b(k)))
+    blocks(WAYS, far_dev, 1, None, lambda k: back_out(k, 1))
+    blocks(WAYS, near_a, 1, back_out(WAYS - 1, 1), lambda k: ret_copy(near_a(k), 1))
+    blocks(WAYS, near_b, 1, ret_copy(near_a(WAYS - 1), 1), lambda k: ret_whole(near_b(k)))
     blocks(1, chip_dev, 1, ret_whole(near_b(WAYS - 1)), None)
     own_block(1, ret_whole(peer(0, 1)))
 

time: 98.7 us -> 98.7 us (level)
  no operation moved by 1% of the time
where the time goes in v15:
time: 98.7 us; the launch traced here: 98.6 us
  Pallas kernels  96.6 us (98%)
  local copies, waits for them, and re-layouts  2.02 us (2%)
    pallas_call x1, Pallas kernels, per_device(): pl.pallas_call(functools.partial(exchange_kernel, n), out_shape=pltpu.VME...  96.6 us
    unnamed x1, local copies, waits for them, and re-layouts  2.02 us

profile of v15, /device:TPU:81, one launch (start us, length us, event | category | flops | bytes accessed | tf_op | source)
XLA Modules:
  0.0 98.6 jit_solution(14808689954253751414)
XLA Ops:
  0.0 96.6 %exchange_sums.1 = bf16[512,4096]{1,0:T(8,128)(2,1)S(1)} custom-call(f32[1,1,512]{2,1,0:T(1,128)} %bitcast.2, s32[1,1,512]{2,1,0:T(1,128)} %bitcast.3, bf16[512,4096]{1,0:T(8,128)(2,1)} %pay_ref.1), custom_call_target="tpu_custom_call" | custom-call | tf_op jit(solution)/shard_map/exchange_sums/pallas_call | solution.py:276
  96.6 2.0 %copy.5 = bf16[512,4096]{1,0:T(8,128)(2,1)} copy(bf16[512,4096]{1,0:T(8,128)(2,1)S(1)} %exchange_sums.1) | data formatting | bytes 8388608

commit v16 on v12

--- a/solution.py
+++ b/solution.py
@@ -110,13 +110,13 @@
     pl.semaphore_wait(barrier, len(near))
     pl.semaphore_signal(far_ok, inc=1, device_id={'group': peer(way(1), 0)}, device_id_type=MESH)
 
-    for dst in near:
-        key_copy(dst).start()
-        seg_copy(dst).start()
     for i in range(WAYS):
         for c in range(CHUNKS):
             pay_copy(far[i], c).wait()
         hop_out(i).start()
+    for dst in near:
+        key_copy(dst).start()
+        seg_copy(dst).start()
     pl.semaphore_wait(far_ok, 1)
     for dst in far:
         key_copy(dst).start()

time: 98.7 us -> 98.7 us (level)
  no operation moved by 1% of the time
where the time goes in v16:
time: 98.7 us; the launch traced here: 98.6 us
  Pallas kernels  96.6 us (98%)
  local copies, waits for them, and re-layouts  2.02 us (2%)
    pallas_call x1, Pallas kernels, per_device(): pl.pallas_call(functools.partial(exchange_kernel, n), out_shape=pltpu.VME...  96.6 us
    unnamed x1, local copies, waits for them, and re-layouts  2.02 us

profile of v16, /device:TPU:81, one launch (start us, length us, event | category | flops | bytes accessed | tf_op | source)
XLA Modules:
  0.0 98.6 jit_solution(17565209839033222094)
XLA Ops:
  0.0 96.6 %exchange_sums.1 = bf16[512,4096]{1,0:T(8,128)(2,1)S(1)} custom-call(f32[1,1,512]{2,1,0:T(1,128)} %bitcast.2, s32[1,1,512]{2,1,0:T(1,128)} %bitcast.3, bf16[512,4096]{1,0:T(8,128)(2,1)} %pay_ref.1), custom_call_target="tpu_custom_call" | custom-call | tf_op jit(solution)/shard_map/exchange_sums/pallas_call | solution.py:276
  96.6 2.0 %copy.5 = bf16[512,4096]{1,0:T(8,128)(2,1)} copy(bf16[512,4096]{1,0:T(8,128)(2,1)S(1)} %exchange_sums.1) | data formatting | bytes 8388608

commit v17 on v12

--- a/solution.py
+++ b/solution.py
@@ -14,6 +14,7 @@
 CHUNKS = 2
 ROW_TILE = 64
 EARLY_STEPS = 8
+STORES = 8
 PARTS = 2
 
 
@@ -265,6 +266,16 @@
         back_on(i).wait_send()
 
 
+def store_kernel(src_ref, dst_ref, sem):
+    rows = src_ref.shape[0] // STORES
+    copies = [pltpu.make_async_copy(src_ref.at[pl.ds(i * rows, rows), :], dst_ref.at[pl.ds(i * rows, rows), :], sem.at[i])
+              for i in range(STORES)]
+    for copy in copies:
+        copy.start()
+    for copy in copies:
+        copy.wait()
+
+
 def solution(mesh):
     n = mesh.shape['group']
 
@@ -273,7 +284,7 @@
         total = n * rows
         dma = pltpu.SemaphoreType.DMA
         block = width // n
-        return pl.pallas_call(
+        result = pl.pallas_call(
             functools.partial(exchange_kernel, n),
             out_shape=pltpu.VMEM((rows, width), jnp.bfloat16),
             in_specs=[pl.BlockSpec(memory_space=pl.ANY)] * 3,
@@ -297,6 +308,15 @@
                                                  vmem_limit_bytes=56 * 1024 * 1024),
             name='exchange_sums',
         )(sort_keys.reshape(1, 1, rows), seg_ids.reshape(1, 1, rows), payload)
+        return pl.pallas_call(
+            store_kernel,
+            out_shape=jax.ShapeDtypeStruct((rows, width), jnp.bfloat16),
+            in_specs=[pl.BlockSpec(memory_space=pl.ANY)],
+            out_specs=pl.BlockSpec(memory_space=pl.ANY),
+            scratch_shapes=[dma((STORES,))],
+            compiler_params=pltpu.CompilerParams(vmem_limit_bytes=1024 * 1024),
+            name='store_result',
+        )(pltpu.with_memory_space_constraint(result, pltpu.VMEM))
 
     row_spec = P(('batch', 'group'))
     mat_spec = P(('batch', 'group'), None)

time: 98.7 us -> 98.8 us (level)
  local copies, waits for them, and re-layouts: 2.02 us -> 0 us
  Pallas kernels: 96.6 us -> 98.6 us
    pallas_call x0 -> x1, Pallas kernels: none -> 2.07 us  [per_device(): pl.pallas_call(store_kernel, out_shape=jax.ShapeDtypeStruct((rows, width)...]
    unnamed x1 -> x0, local copies, waits for them, and re-layouts: 2.02 us -> none
where the time goes in v17:
time: 98.8 us; the launch traced here: 98.6 us
  Pallas kernels  98.6 us (100%)
    pallas_call x1, Pallas kernels, per_device(): pl.pallas_call(functools.partial(exchange_kernel, n), out_shape=pltpu.VME...  96.6 us
    pallas_call x1, Pallas kernels, per_device(): pl.pallas_call(store_kernel, out_shape=jax.ShapeDtypeStruct((rows, width)...  2.07 us

profile of v17, /device:TPU:81, one launch (start us, length us, event | category | flops | bytes accessed | tf_op | source)
XLA Modules:
  0.0 98.6 jit_solution(17363316170841223288)
XLA Ops:
  0.0 96.6 %exchange_sums.1.src_ref = bf16[512,4096]{1,0:T(8,128)(2,1)S(1)} custom-call(f32[1,1,512]{2,1,0:T(1,128)} %bitcast.2, s32[1,1,512]{2,1,0:T(1,128)} %bitcast.3, bf16[512,4096]{1,0:T(8,128)(2,1)} %pay_ref.1), custom_call_target="tpu_custom_call" | custom-call | tf_op jit(solution)/shard_map/exchange_sums/pallas_call | solution.py:287
  96.6 2.1 %store_result.1 = bf16[512,4096]{1,0:T(8,128)(2,1)} custom-call(bf16[512,4096]{1,0:T(8,128)(2,1)S(1)} %exchange_sums.1.src_ref), custom_call_target="tpu_custom_call" | custom-call | tf_op jit(solution)/shard_map/store_result/pallas_call | solution.py:311

commit v18 on v12

--- a/solution.py
+++ b/solution.py
@@ -13,7 +13,7 @@
 WAYS = 2
 CHUNKS = 2
 ROW_TILE = 64
-EARLY_STEPS = 8
+EARLY_STEPS = 4
 PARTS = 2
 
 

time: 98.7 us -> 98.7 us (level)
  no operation moved by 1% of the time
where the time goes in v18:
time: 98.7 us; the launch traced here: 98.6 us
  Pallas kernels  96.6 us (98%)
  local copies, waits for them, and re-layouts  2.02 us (2%)
    pallas_call x1, Pallas kernels, per_device(): pl.pallas_call(functools.partial(exchange_kernel, n), out_shape=pltpu.VME...  96.6 us
    unnamed x1, local copies, waits for them, and re-layouts  2.02 us

profile of v18, /device:TPU:81, one launch (start us, length us, event | category | flops | bytes accessed | tf_op | source)
XLA Modules:
  0.0 98.6 jit_solution(8959688137186010571)
XLA Ops:
  0.0 96.6 %exchange_sums.1 = bf16[512,4096]{1,0:T(8,128)(2,1)S(1)} custom-call(f32[1,1,512]{2,1,0:T(1,128)} %bitcast.2, s32[1,1,512]{2,1,0:T(1,128)} %bitcast.3, bf16[512,4096]{1,0:T(8,128)(2,1)} %pay_ref.1), custom_call_target="tpu_custom_call" | custom-call | tf_op jit(solution)/shard_map/exchange_sums/pallas_call | solution.py:276
  96.6 2.0 %copy.5 = bf16[512,4096]{1,0:T(8,128)(2,1)} copy(bf16[512,4096]{1,0:T(8,128)(2,1)S(1)} %exchange_sums.1) | data formatting | bytes 8388608
